TPU v7x, 32 devices: a whole 2x2x4 slice. The times are simulated.
32 devices in a mesh: data: 32 (over z, y, x, core).
Axes of the slice: x: 2, y: 2, z: 4, core: 2. Of those that a mesh axis runs over, the one named last changes fastest.
Arguments:
- w_in: float32 [4096, 512], replicated
- w_up: float32 [12, 512, 2048], replicated
- w_down: float32 [12, 2048, 512], replicated
- mom_in: float32 [4096, 512], replicated
- mom_up: float32 [12, 512, 2048], replicated
- mom_down: float32 [12, 2048, 512], replicated
- x_now: bfloat16 [8192, 4096], P('data')
- y_now: bfloat16 [8192, 512], P('data')
- x_next: bfloat16 [8192, 4096], P('data')
- y_next: bfloat16 [8192, 512], P('data')
Outputs:
- output 1: float32 [4096, 512], replicated
- output 2: float32 [12, 512, 2048], replicated
- output 3: float32 [12, 2048, 512], replicated
- output 4: float32 [4096, 512], replicated
- output 5: float32 [12, 512, 2048], replicated
- output 6: float32 [12, 2048, 512], replicated
- output 7: float32 [8192], P('data')
- output 8: float32 [8192, 512], P('data')
All inputs are finite; a program needn't handle non-finite values.
Results may differ from a plain program's by a relative error of at most 0.0119842.
Values are sent between devices in bfloat16 or wider.
A program may use at most 1.75 GiB of HBM per device.

v0:
```python
import jax
import jax.numpy as jnp
from jax import lax
from jax.sharding import PartitionSpec as P

MOMENTUM = 0.9
ROW_CONTRACT = (((0,), (0,)), ((), ()))
COL_CONTRACT = (((1,), (1,)), ((), ()))


def gelu_tanh(pre_value):
    return jax.nn.gelu(pre_value, approximate=True)


def stack_forward(x_rows, in_low, up_low, down_low):
    h_state = jnp.dot(x_rows, in_low, preferred_element_type=jnp.float32)
    saved_acts = []
    for layer_idx in range(up_low.shape[0]):
        h_low = h_state.astype(jnp.bfloat16)
        pre_act = jnp.dot(h_low, up_low[layer_idx], preferred_element_type=jnp.float32)
        act_val, gelu_back = jax.vjp(gelu_tanh, pre_act)
        act_low = act_val.astype(jnp.bfloat16)
        h_state = h_state + jnp.dot(act_low, down_low[layer_idx], preferred_element_type=jnp.float32)
        saved_acts.append((h_low, act_low, gelu_back))
    return h_state, saved_acts


def solution(mesh):
    group_size = mesh.shape["data"]

    def device_steps(w_in, w_up, w_down, mom_in, mom_up, mom_down, x_now, y_now, x_next, y_next):
        local_rows, model_width = y_now.shape
        layer_count = w_up.shape[0]
        step_size = 4.0 * model_width / (w_up.shape[2] * (layer_count + 1))
        up_low = w_up.astype(jnp.bfloat16)
        down_low = w_down.astype(jnp.bfloat16)
        h_last, saved_acts = stack_forward(x_now, w_in.astype(jnp.bfloat16), up_low, down_low)
        cot_state = (h_last - y_now.astype(jnp.float32)) / (local_rows * group_size * model_width)
        grads_up = [None] * layer_count
        grads_down = [None] * layer_count
        for layer_idx in reversed(range(layer_count)):
            h_low, act_low, gelu_back = saved_acts[layer_idx]
            cot_low = cot_state.astype(jnp.bfloat16)
            local_down = lax.dot_general(act_low, cot_low, ROW_CONTRACT, preferred_element_type=jnp.float32)
            grads_down[layer_idx] = lax.psum(local_down.astype(jnp.bfloat16), "data")
            act_cot = lax.dot_general(cot_low, down_low[layer_idx], COL_CONTRACT, preferred_element_type=jnp.float32)
            pre_cot = gelu_back(act_cot)[0].astype(jnp.bfloat16)
            local_up = lax.dot_general(h_low, pre_cot, ROW_CONTRACT, preferred_element_type=jnp.float32)
            grads_up[layer_idx] = lax.psum(local_up.astype(jnp.bfloat16), "data")
            cot_state = cot_state + lax.dot_general(pre_cot, up_low[layer_idx], COL_CONTRACT, preferred_element_type=jnp.float32)
        local_in = lax.dot_general(x_now, cot_state.astype(jnp.bfloat16), ROW_CONTRACT, preferred_element_type=jnp.float32)
        grad_in = lax.psum(local_in.astype(jnp.bfloat16), "data")
        new_mom_in = MOMENTUM * mom_in + grad_in.astype(jnp.float32)
        new_mom_up = MOMENTUM * mom_up + jnp.stack(grads_up).astype(jnp.float32)
        new_mom_down = MOMENTUM * mom_down + jnp.stack(grads_down).astype(jnp.float32)
        new_w_in = w_in - step_size * new_mom_in
        new_w_up = w_up - step_size * new_mom_up
        new_w_down = w_down - step_size * new_mom_down
        h_next = stack_forward(x_next, new_w_in.astype(jnp.bfloat16), new_w_up.astype(jnp.bfloat16), new_w_down.astype(jnp.bfloat16))[0]
        loss_next = jnp.sum(jnp.square(h_next - y_next.astype(jnp.float32)), axis=1) / (2 * model_width)
        return (new_w_in, new_w_up, new_w_down, new_mom_in, new_mom_up, new_mom_down, loss_next, h_next)

    param_spec = P()
    row_spec = P("data", None)
    return jax.shard_map(
        device_steps,
        mesh=mesh,
        in_specs=(param_spec,) * 6 + (row_spec,) * 4,
        out_specs=(param_spec,) * 6 + (P("data"), row_spec),
        check_vma=False,
    )
```

profile of v0, /device:TPU:0, one launch (start us, length us, event | category | flops | bytes accessed | tf_op | source)
XLA Modules:
  0.0 2966.1 jit_solution(13255564242664492446)
XLA Ops:
  7.2 26.0 convert_element_type.332
  33.3 25.6 convert_element_type.334
  58.9 4.6 fusion.3
  133.8 4.2 fusion.26
  138.0 4.9 fusion.98
  148.9 4.9 fusion.91
  155.8 4.0 fusion.24
  159.8 4.9 fusion.84
  170.7 4.9 fusion.77
  181.8 4.9 fusion.70
  192.7 4.9 fusion.63
  202.0 4.3 fusion.56
  247.6 4.3 fusion.35
  251.9 6.0 fusion
  261.2 8.9 copy.19
  270.1 8.9 copy.18
  279.9 2379.6 %all-reduce.3.cloned.1.call-done = (bf16[4096,512]{0,1:T(8,128)(2,1)}, bf16[1,512,2048]{2,1,0:T(8,128)(2,1)}, bf16[1,512,2048]{2,1,0:T(8,128)(2,1)}, bf16[1,512,...) async-done(((bf16[4096,512]{0,1:T(8,128)(2,1)}, ...) | async-done | bytes 54525968 | tf_op jit(solution)/shard_map/psum | solution.py:52
  2666.5 10.1 multiply_subtract_fusion.2
  2676.6 8.9 copy.33
  2685.5 6.2 fusion.281
  2716.7 79.0 %fusion.444 = (bf16[12,2048,512]{2,1,0:T(8,128)(2,1)}, f32[12,2048,512]{2,1,0:T(8,128)}, f32[12,2048,512]{2,1,0:T(8,128)}) fusion(f32[12,2048,512]{2,1,0:T(8,128)} %param.12, bf16[12,2048,512]{2,1,0:T(8,128)(2,1)} %constant_dynamic-update-slice_fusion.12, f32[12,2048,512]{2,1,0:T(8,128)} %param.15), kind=kLoop, calls=%fused_computation.583 | loop fusion | flops 75497472 | bytes 251658240 | tf_op jit(solution)/shard_map/convert_element_type | solution.py:59
  2820.8 79.9 %fusion.443 = (bf16[12,512,2048]{2,1,0:T(8,128)(2,1)}, f32[12,512,2048]{2,1,0:T(8,128)}, f32[12,512,2048]{2,1,0:T(8,128)}) fusion(f32[12,512,2048]{2,1,0:T(8,128)} %param.11, bf16[12,512,2048]{2,1,0:T(8,128)(2,1)} %constant_dynamic-update-slice_fusion, f32[12,512,2048]{2,1,0:T(8,128)} %param.14), kind=kLoop, calls=%fused_computation.582 | loop fusion | flops 75497472 | bytes 251658240 | tf_op jit(solution)/shard_map/convert_element_type | solution.py:59
  2928.4 4.2 fusion.316
  2950.0 9.1 copy.34
  (193 shorter events, 247.7 us)
Async XLA Ops:
  7.2 51.8 %copy-start = (bf16[256,4096]{1,0:T(8,128)(2,1)S(1)}, bf16[256,4096]{1,0:T(8,128)(2,1)}, u32[]{:S(2)}) copy-start(bf16[256,4096]{1,0:T(8,128)(2,1)} %param.16) | copy-start | bytes 6291460
  7.2 2652.4 %all-reduce.3.cloned.1.call-start = ((), (), s32[]{:S(2)}) async-start(), calls=%async_computation | async-start | bytes 109051904 | tf_op jit(solution)/shard_map/psum | solution.py:52
  63.5 11.5 copy-start.2
  82.0 3.2 copy-start.26
  85.9 3.3 copy-start.27
  89.9 3.2 copy-start.28
  93.8 3.2 copy-start.29
  103.3 3.2 copy-start.30
  199.6 2.4 copy-start.45
  210.9 3.9 copy-start.35
  270.1 8.9 copy-start.42
  2659.5 6.9 copy-start.3
  2685.5 6.2 copy-start.25
  2691.7 2.3 copy-start.24
  2694.1 2.3 copy-start.23
  2696.4 2.3 copy-start.22
  2698.8 2.3 copy-start.21
  2701.1 2.3 copy-start.20
  2703.5 2.3 copy-start.19
  2716.7 79.0 %copy-start.14 = (bf16[1,512,2048]{2,1,0:T(8,128)(2,1)S(1)}, bf16[1,512,2048]{2,1,0:T(8,128)(2,1)}, u32[]{:S(2)}) copy-start(bf16[1,512,2048]{2,1,0:T(8,128)(2,1)} %get-tuple-element.18) | copy-start | bytes 6291460
  2795.7 2.3 copy-start.13
  2820.8 79.9 %copy-start.32 = (f32[256,512]{0,1:T(8,128)S(1)}, f32[256,512]{0,1:T(8,128)}, u32[]{:S(2)}) copy-start(f32[256,512]{0,1:T(8,128)} %fusion.281) | copy-start | bytes 1572868
  2940.4 4.0 copy-start.43
  2950.0 9.1 copy-start.1
  (23 other events, 49.5 us)
Sparse Core Ops, SparseCore 0:
  261.3 2398.1 all-reduce.2
where the time goes:
time: 2980 us; the launch traced here: 2970 us
  waiting for transfers between devices  2380 us (80%)
  matrix products  254 us (9%)
  other arithmetic  221 us (7%)
  local copies, waits for them, and re-layouts  96.3 us (3%)
    psum x1, waiting for transfers between devices, device_steps(): grad_in = lax.psum(local_in.astype(jnp.bfloat16), 'data')  2380 us
    unnamed x120, local copies, waits for them, and re-layouts  93.2 us
    dot_general x24, matrix products, stack_forward(): jnp.dot(act_low, down_low[layer_idx], preferred_element_type=jnp.float32)  82.9 us
    convert_element_type x1, other arithmetic, device_steps(): new_w_up.astype(jnp.bfloat16)  79.9 us
    convert_element_type x1, other arithmetic, device_steps(): new_w_down.astype(jnp.bfloat16)  79 us
  transfers between devices with their start and end apart: 1, of which 1 were waited for; matrix products, arithmetic and copies ran while one was open for 1% of the time, Pallas kernels for 0%

commit v1 on v0

v1 whole, which is shorter than its diff:
```python
import functools

import jax
import jax.numpy as jnp
from jax import lax
from jax.experimental import pallas as pl
from jax.experimental.pallas import tpu as pltpu
from jax.sharding import PartitionSpec as P

MOMENTUM = 0.9
MESH = pl.DeviceIdType.MESH
BIT = {"c": 1, "x": 2, "y": 4, "a": 8, "b": 16}

def ar_kernel(nu, tr, tw, lags, orders, *refs):
    (g, gs, acc, fin, rb0, rb1, rb2, rb3, rb4, ld_s, c_s, c_r, rs_s, rs_r, ag_s, ag_r, d_s, d_r, st_s) = refs
    K = ld_s.shape[0]
    NS, NF = acc.shape[0], fin.shape[0]
    l0, lrs, lag_, ld = lags
    me = lax.axis_index("data")
    bit = {d: lax.rem(me // BIT[d], 2) for d in BIT}
    peer = {d: me + BIT[d] * (1 - 2 * bit[d]) for d in BIT}
    bar = pltpu.get_barrier_semaphore()
    for d in "cxyab":
        pl.semaphore_signal(bar, inc=1, device_id=(peer[d],), device_id_type=MESH)
    pl.semaphore_wait(bar, 5)
    half = tr // 2
    rbs = [None, rb1, rb2, rb3, rb4]
    base, size = [], [half >> s for s in range(5)]
    for k, od in enumerate(orders):
        b = [k * half]
        for s, d in enumerate(od):
            b.append(b[-1] + size[s + 1] * bit[d])
        base.append(b)
    give = [[base[k][s] + size[s + 1] * (1 - bit[d]) for s, d in enumerate(od)] for k, od in enumerate(orders)]
    o = [0, l0]
    for s in range(4): o.append(o[-1] + lrs[s])
    for s in range(4): o.append(o[-1] + lag_[s])
    o.append(o[-1] + ld)
    assert NS >= o[5] and NF >= o[10] - o[1]
    AL = min(16, half // 16)
    def rows(off, n):
        return pl.ds(pl.multiple_of(off, AL), n)
    def cp_load(u):
        return pltpu.make_async_copy(g.at[u, bit["c"]], acc.at[lax.rem(u, NS)], ld_s.at[lax.rem(u, K)])
    def cp_c(u):
        return pltpu.make_async_remote_copy(src_ref=g.at[u, 1 - bit["c"]], dst_ref=rb0.at[lax.rem(u, K)],
            send_sem=c_s.at[lax.rem(u, K)], recv_sem=c_r.at[lax.rem(u, K)], device_id=(peer["c"],), device_id_type=MESH)
    def cp_rs(u, k, s):
        return pltpu.make_async_remote_copy(src_ref=acc.at[lax.rem(u, NS), rows(give[k][s - 1], size[s])], dst_ref=rbs[s].at[k, lax.rem(u, K)],
            send_sem=rs_s.at[s - 1, k, lax.rem(u, K)], recv_sem=rs_r.at[s - 1, k, lax.rem(u, K)],
            device_id=(peer[orders[k][s - 1]],), device_id_type=MESH)
    def cp_ag(u, k, s):
        sl = fin.at[lax.rem(u, NF), rows(base[k][s], size[s])]
        return pltpu.make_async_remote_copy(src_ref=sl, dst_ref=sl, send_sem=ag_s.at[s - 1, k, lax.rem(u, K)], recv_sem=ag_r.at[s - 1, k, lax.rem(u, K)],
            device_id=(peer[orders[k][s - 1]],), device_id_type=MESH)
    def cp_d(u):
        return pltpu.make_async_remote_copy(src_ref=fin.at[lax.rem(u, NF)], dst_ref=gs.at[u, bit["c"]],
            send_sem=d_s.at[lax.rem(u, K)], recv_sem=d_r.at[lax.rem(u, K)], device_id=(peer["c"],), device_id_type=MESH)
    def cp_st(u):
        return pltpu.make_async_copy(fin.at[lax.rem(u, NF)], gs.at[u, bit["c"]], st_s.at[lax.rem(u, K)])
    def add_c(u):
        sl = lax.rem(u, NS)
        for h in range(4):
            r = slice(h * tr // 4, (h + 1) * tr // 4)
            acc[sl, r] = (acc[sl, r].astype(jnp.float32) + rb0[lax.rem(u, K), r].astype(jnp.float32)).astype(jnp.bfloat16)
    def add_rs(u, k, s):
        sl = lax.rem(u, NS)
        r = rows(base[k][s], size[s])
        out, so = (fin, lax.rem(u, NF)) if s == 4 else (acc, sl)
        out[so, r] = (acc[sl, r].astype(jnp.float32) + rbs[s][k, lax.rem(u, K)].astype(jnp.float32)).astype(jnp.bfloat16)

    def tick(t, _):
        def ev(e, f):
            u = t - o[e]
            @pl.when(jnp.logical_and(u >= 0, u < nu))
            def _():
                f(u)
        def e10(u):
            cp_d(u).wait(); cp_st(u).wait()
        def e9(u):
            for k in range(2): cp_ag(u, k, 1).wait()
            cp_d(u).start(); cp_st(u).start()
        def mk_ag(s):
            def f(u):
                for k in range(2): cp_ag(u, k, s).wait()
                for k in range(2): cp_ag(u, k, s - 1).start()
            return f
        def e5(u):
            for k in range(2):
                cp_rs(u, k, 4).wait(); add_rs(u, k, 4)
            for k in range(2): cp_ag(u, k, 4).start()
        def mk_rs(s):
            def f(u):
                for k in range(2):
                    cp_rs(u, k, s - 1).wait(); add_rs(u, k, s - 1)
                for k in range(2): cp_rs(u, k, s).start()
            return f
        def e1(u):
            cp_load(u).wait(); cp_c(u).wait(); add_c(u)
            for k in range(2): cp_rs(u, k, 1).start()
        def e0(u):
            cp_load(u).start(); cp_c(u).start()
        ev(10, e10); ev(9, e9)
        for e, s in ((8, 2), (7, 3), (6, 4)): ev(e, mk_ag(s))
        ev(5, e5)
        for e in (4, 3, 2): ev(e, mk_rs(e))
        ev(1, e1); ev(0, e0)
        return 0
    lax.fori_loop(0, nu + o[10], tick, 0)

def all_reduce(g, lags=(1, (2, 2, 2, 2), (2, 2, 2, 2), 1), orders=("xayb", "yaxb"), cid=0):
    nu, _, tr, tw = g.shape
    l0, lrs, lag_, ld = lags
    K = 2 * max(l0, ld, *lrs, *lag_)
    NS = l0 + sum(lrs)
    NF = sum(lrs) + sum(lag_) + ld
    bf = jnp.bfloat16
    half = tr // 2
    return pl.pallas_call(
        functools.partial(ar_kernel, nu, tr, tw, lags, orders),
        out_shape=jax.ShapeDtypeStruct(g.shape, bf),
        in_specs=[pl.BlockSpec(memory_space=pl.ANY)],
        out_specs=pl.BlockSpec(memory_space=pl.ANY),
        scratch_shapes=[pltpu.VMEM((NS, tr, tw), bf), pltpu.VMEM((NF, tr, tw), bf), pltpu.VMEM((K, tr, tw), bf)]
        + [pltpu.VMEM((2, K, half >> s, tw), bf) for s in range(1, 5)]
        + [pltpu.SemaphoreType.DMA((K,))] * 3 + [pltpu.SemaphoreType.DMA((4, 2, K))] * 4 + [pltpu.SemaphoreType.DMA((K,))] * 3,
        compiler_params=pltpu.CompilerParams(collective_id=cid, has_side_effects=True, vmem_limit_bytes=56 * 2**20),
        name="grad_sum",
    )(g)

bf, f32 = jnp.bfloat16, jnp.float32
TN = (((0,), (0,)), ((), ()))
NT = (((1,), (1,)), ((), ()))
def dot(a, b): return jnp.dot(a, b, preferred_element_type=f32)
def gelu_tanh(v): return jax.nn.gelu(v, approximate=True)

def fwd_kernel(layers, x, w_in, w_up, w_down, p_out, h_out, h):
    i = pl.program_id(0)
    @pl.when(i < 4)
    def _():
        kq = x.shape[1]
        part = dot(x[...], w_in[...].astype(bf))
        @pl.when(i == 0)
        def _(): h[...] = part
        @pl.when(i > 0)
        def _(): h[...] += part
    @pl.when(i >= 4)
    def _():
        p = h[...].astype(bf)
        p_out[0] = p
        n = w_up.shape[2] // 4
        for q in range(4):
            c = slice(q * n, (q + 1) * n)
            u = dot(p, w_up[0, :, c].astype(bf))
            a = gelu_tanh(u).astype(bf)
            h[...] += dot(a, w_down[0, c, :].astype(bf))
    @pl.when(i == layers + 3)
    def _(): h_out[...] = h[...]

def forward(x, w_in, w_up, w_down):
    rows, e = x.shape
    layers, d, ff = w_up.shape
    lay = lambda i: jnp.maximum(i - 4, 0)
    return pl.pallas_call(
        functools.partial(fwd_kernel, layers), grid=(layers + 4,),
        out_shape=[jax.ShapeDtypeStruct((layers, rows, d), bf), jax.ShapeDtypeStruct((rows, d), f32)],
        in_specs=[pl.BlockSpec((rows, e // 4), lambda i: (0, jnp.minimum(i, 3))), pl.BlockSpec((e // 4, d), lambda i: (jnp.minimum(i, 3), 0)),
                  pl.BlockSpec((1, d, ff), lambda i: (lay(i), 0, 0)), pl.BlockSpec((1, ff, d), lambda i: (lay(i), 0, 0))],
        out_specs=[pl.BlockSpec((1, rows, d), lambda i: (lay(i), 0, 0)), pl.BlockSpec((rows, d), lambda i: (0, 0))],
        scratch_shapes=[pltpu.VMEM((rows, d), f32)],
        compiler_params=pltpu.CompilerParams(vmem_limit_bytes=60 * 2**20), name="forward",
    )(x, w_in, w_up, w_down)

def bwd_kernel(layers, scale, x, y, h_last, p, w_up, w_down, g, c_state):
    i = pl.program_id(0)
    d, ff = w_up.shape[1:]
    @pl.when(i == 0)
    def _(): c_state[...] = (h_last[...] - y[...].astype(f32)) / scale
    @pl.when(i < layers)
    def _():
        c_low = c_state[...].astype(bf)
        pl_ = p[0]
        n = ff // 4
        for q in range(4):
            c = slice(q * n, (q + 1) * n)
            wu = w_up[0, :, c].astype(bf)
            u = dot(pl_, wu)
            act, back = jax.vjp(gelu_tanh, u)
            a = act.astype(bf)
            ac = lax.dot_general(c_low, w_down[0, c, :].astype(bf), NT, preferred_element_type=f32)
            pre = back(ac)[0].astype(bf)
            gd = lax.dot_general(a, c_low, TN, preferred_element_type=f32).astype(bf)
            gu = lax.dot_general(pl_, pre, TN, preferred_element_type=f32).astype(bf)
            g[q, 0] = gu[:, :n // 2]
            g[q, 1] = gu[:, n // 2:]
            for j in range(2):
                g[4 + 2 * (q // 2) + j, q % 2] = gd[:, j * (d // 2):(j + 1) * (d // 2)]
            c_state[...] += lax.dot_general(pre, wu, NT, preferred_element_type=f32)
    @pl.when(i == layers)
    def _():
        c_low = c_state[...].astype(bf)
        for q in range(8):
            gi = lax.dot_general(x[:, q * 512:(q + 1) * 512], c_low, TN, preferred_element_type=f32).astype(bf)
            for j in range(2):
                g[2 * (q // 2) + j, q % 2] = gi[:, j * (d // 2):(j + 1) * (d // 2)]

def backward(scale, x, y, h_last, p, w_up, w_down):
    rows, e = x.shape
    layers, d, ff = w_up.shape
    lay = lambda i: jnp.maximum(layers - 1 - i, 0)
    nu = 8 * (layers + 1)
    return pl.pallas_call(
        functools.partial(bwd_kernel, layers, scale), grid=(layers + 1,),
        out_shape=jax.ShapeDtypeStruct((nu, 2, 512, d // 2), bf),
        in_specs=[pl.BlockSpec((rows, e), lambda i: (0, 0)), pl.BlockSpec((rows, d), lambda i: (0, 0)), pl.BlockSpec((rows, d), lambda i: (0, 0)),
                  pl.BlockSpec((1, rows, d), lambda i: (lay(i), 0, 0)),
                  pl.BlockSpec((1, d, ff), lambda i: (lay(i), 0, 0)), pl.BlockSpec((1, ff, d), lambda i: (lay(i), 0, 0))],
        out_specs=pl.BlockSpec((8, 2, 512, d // 2), lambda i: (layers - i, 0, 0, 0)),
        scratch_shapes=[pltpu.VMEM((rows, d), f32)],
        compiler_params=pltpu.CompilerParams(vmem_limit_bytes=60 * 2**20), name="backward",
    )(x, y, h_last, p, w_up, w_down)

def upd_kernel(layers, eta, mu, x, y, g, w_in, w_up, w_down, m_in, m_up, m_down,
               nw_in, nw_up, nw_down, nm_in, nm_up, nm_down, loss, h_out, h, p, a):
    i = pl.program_id(0)
    d = h.shape[1]
    d2 = d // 2
    v = i - 8
    r = lax.rem(jnp.maximum(v, 0), 8)
    def upd(w, m, nw, nm, t, ix):
        nmv = mu * m[ix] + g[0, t].astype(f32)
        nm[ix] = nmv
        nwv = w[ix] - eta * nmv
        nw[ix] = nwv
        return nwv.astype(bf)
    @pl.when(i < 8)
    def _():
        j = lax.rem(i, 2)
        cols = pl.ds(pl.multiple_of(j * d2, d2), d2)
        tot = None
        for t in range(2):
            s = slice(512 * t, 512 * (t + 1))
            wl = upd(w_in, m_in, nw_in, nm_in, t, (s, slice(None)))
            q = dot(x[:, s], wl)
            tot = q if tot is None else tot + q
        @pl.when(i < 2)
        def _(): h[:, cols] = tot
        @pl.when(i >= 2)
        def _(): h[:, cols] += tot
    @pl.when(jnp.logical_and(v >= 0, r == 0))
    def _(): p[...] = h[...].astype(bf)
    @pl.when(jnp.logical_and(v >= 0, r < 4))
    def _():
        for t in range(2):
            s = slice(d2 * t, d2 * (t + 1))
            wl = upd(w_up, m_up, nw_up, nm_up, t, (0, slice(None), s))
            u = dot(p[...], wl)
            a[r, :, s] = gelu_tanh(u).astype(bf)
    @pl.when(jnp.logical_and(v >= 0, r >= 4))
    def _():
        j = lax.rem(r, 2)
        ig = (r - 4) // 2
        cols = pl.ds(pl.multiple_of(j * d2, d2), d2)
        tot = None
        for t in range(2):
            s = slice(512 * t, 512 * (t + 1))
            wl = upd(w_down, m_down, nw_down, nm_down, t, (0, s, slice(None)))
            q = dot(a[2 * ig + t], wl)
            tot = q if tot is None else tot + q
        h[:, cols] += tot
    @pl.when(i == 8 * layers + 7)
    def _():
        h_out[...] = h[...]
        e = h[...] - y[...].astype(f32)
        loss[...] = jnp.sum(e * e, axis=1, keepdims=True) / (2 * d)

def update(eta, mu, x, y, g, w_in, w_up, w_down, m_in, m_up, m_down):
    rows, e = x.shape
    layers, d, ff = w_up.shape
    nu = 8 * (layers + 1)
    def ii(i):
        u = jnp.minimum(i, 7); return (u // 2, lax.rem(u, 2))
    def iu(i):
        v = jnp.maximum(i - 8, 0); return (v // 8, 0, jnp.minimum(lax.rem(v, 8), 3))
    def idn(i):
        v = jnp.maximum(i - 8, 0); q = jnp.maximum(lax.rem(v, 8) - 4, 0); return (v // 8, q // 2, lax.rem(q, 2))
    s_in = pl.BlockSpec((1024, d // 2), ii)
    s_up = pl.BlockSpec((1, d, 512), iu)
    s_dn = pl.BlockSpec((1, 1024, d // 2), idn)
    x_spec = pl.BlockSpec((rows, 1024), lambda i: (0, jnp.minimum(i, 7) // 2))
    full = pl.BlockSpec((rows, d), lambda i: (0, 0))
    o = [jax.ShapeDtypeStruct(t.shape, f32) for t in (w_in, w_up, w_down, m_in, m_up, m_down)]
    o += [jax.ShapeDtypeStruct((rows, 1), f32), jax.ShapeDtypeStruct((rows, d), f32)]
    return pl.pallas_call(
        functools.partial(upd_kernel, layers, eta, mu), grid=(nu,), out_shape=o,
        in_specs=[x_spec, full, pl.BlockSpec((1, 2, 512, d // 2), lambda i: (i, 0, 0, 0)), s_in, s_up, s_dn, s_in, s_up, s_dn],
        out_specs=[s_in, s_up, s_dn, s_in, s_up, s_dn, pl.BlockSpec((rows, 1), lambda i: (0, 0)), full],
        scratch_shapes=[pltpu.VMEM((rows, d), f32), pltpu.VMEM((rows, d), bf), pltpu.VMEM((4, rows, 512), bf)],
        compiler_params=pltpu.CompilerParams(vmem_limit_bytes=60 * 2**20), name="update",
    )(x, y, g, w_in, w_up, w_down, m_in, m_up, m_down)


def solution(mesh):
    group_size = mesh.shape["data"]

    def device_steps(w_in, w_up, w_down, mom_in, mom_up, mom_down, x_now, y_now, x_next, y_next):
        local_rows, model_width = y_now.shape
        step_size = 4.0 * model_width / (w_up.shape[2] * (w_up.shape[0] + 1))
        p_all, h_last = forward(x_now, w_in, w_up, w_down)
        local = backward(float(local_rows * group_size * model_width), x_now, y_now, h_last, p_all, w_up, w_down)
        total = all_reduce(local, lags=(1, (3, 3, 3, 3), (3, 3, 3, 3), 1))
        out = update(step_size, MOMENTUM, x_next, y_next, total, w_in, w_up, w_down, mom_in, mom_up, mom_down)
        return (*out[:6], out[6][:, 0], out[7])

    row_spec = P("data", None)
    return jax.shard_map(
        device_steps,
        mesh=mesh,
        in_specs=(P(),) * 6 + (row_spec,) * 4,
        out_specs=(P(),) * 6 + (P("data"), row_spec),
        check_vma=False,
    )
```

time: 2980 us -> 705 us (0.24)
  waiting for transfers between devices: 2380 us -> 0 us
  Pallas kernels: 0 us -> 701 us
  matrix products: 254 us -> 0 us
  other arithmetic: 221 us -> 1.58 us
  local copies, waits for them, and re-layouts: 96.3 us -> 0 us
    psum x1 -> x0, waiting for transfers between devices: 2380 us -> none  [device_steps(): grad_in = lax.psum(local_in.astype(jnp.bfloat16), 'data')]
    pallas_call x0 -> x4, Pallas kernels: none -> 701 us  [the longest x1 404 us: all_reduce(): pl.pallas_call(functools.partial(ar_kernel, nu, tr, tw, lags, orders), ou...]
    dot_general x86 -> x0, matrix products: 254 us -> none  [the longest x24 82.9 us: stack_forward(): jnp.dot(act_low, down_low[layer_idx], preferred_element_type=jnp.float32)]
    convert_element_type x4 -> x0, other arithmetic: 211 us -> none  [the longest x1 79.9 us: device_steps(): new_w_up.astype(jnp.bfloat16)]
    unnamed x120 -> x0, local copies, waits for them, and re-layouts: 93.2 us -> none
  transfers between devices with their start and end apart: 1 -> 0, of which waited for: 1 -> 0; matrix products, arithmetic and copies ran while one was open for 1% -> 0% of each run, Pallas kernels for 0% -> 0%
where the time goes in v1:
time: 705 us; the launch traced here: 703 us
  Pallas kernels  701 us (99%)
    pallas_call x1, Pallas kernels, all_reduce(): pl.pallas_call(functools.partial(ar_kernel, nu, tr, tw, lags, orders), ou...  404 us
    pallas_call x1, Pallas kernels, update(): pl.pallas_call(functools.partial(upd_kernel, layers, eta, mu), grid=(nu,)...  192 us
    pallas_call x1, Pallas kernels, backward(): pl.pallas_call(functools.partial(bwd_kernel, layers, scale), grid=(layers...  62.8 us
    pallas_call x1, Pallas kernels, forward(): pl.pallas_call(functools.partial(fwd_kernel, layers), grid=(layers + 4,),...  42.1 us

profile of v1, /device:TPU:0, one launch (start us, length us, event | category | flops | bytes accessed | tf_op | source)
XLA Modules:
  0.0 703.3 jit_solution(7149653684224756269)
XLA Ops:
  0.6 42.1 %forward.1 = (bf16[12,256,512]{2,1,0:T(8,128)(2,1)}, f32[256,512]{1,0:T(8,128)}) custom-call(bf16[256,4096]{1,0:T(8,128)(2,1)} %x.4, f32[4096,512]{1,0:T(8,128)} %w_in.3, f32[12,512,2048]{2,1,0:T(8,128)} %w_up.5, f32[12,2048,512]{2,1,0:T(8,128)} %w_down.5), custom_call_target="tpu_custom_call" | custom-call | tf_op jit(solution)/shard_map/forward/pallas_call | solution.py:164
  42.7 62.8 %backward.1.refs_0_ = bf16[104,2,512,256]{3,2,1,0:T(8,128)(2,1)} custom-call(bf16[256,4096]{1,0:T(8,128)(2,1)} %x.4, bf16[256,512]{1,0:T(8,128)(2,1)} %y.2, f32[256,512]{1,0:T(8,128)} %get-tuple-element.18.h_last, bf16[12,256,512]{2,1,0:T(8,128)(2,1)} %get-tuple-element.19.p, f32[12,512,2048]{2,1,0:T(8,128)} %w_up.5, f32[12,2048,512]{2,1,0:T(8,128)} %w_down.5), custom_call_target="tpu_custom_call" | custom-call | tf_op jit(solution)/shard_map/backward/pallas_call | solution.py:212
  105.5 403.9 %grad_sum.1.g = bf16[104,2,512,256]{3,2,1,0:T(8,128)(2,1)} custom-call(bf16[104,2,512,256]{3,2,1,0:T(8,128)(2,1)} %backward.1.refs_0_), custom_call_target="tpu_custom_call" | custom-call | tf_op jit(solution)/shard_map/grad_sum/pallas_call | solution.py:119
  509.3 192.4 %update.1 = (f32[4096,512]{1,0:T(8,128)}, f32[12,512,2048]{2,1,0:T(8,128)}, f32[12,2048,512]{2,1,0:T(8,128)}, f32[4096,512]{1,0:T(8,128)}, f32[12,512,2048]{2,1,...) custom-call(bf16[256,4096]{1,0:T(8,128)(2,1)} %x.5, bf16[256,512]{1,0:T(8,128)(2,1)} %y.3, ...), custom_call_target="tpu_custom_call" | custom-call | tf_op jit(solution)/shard_map/update/pallas_call | solution.py:294
  701.7 1.6 reduce

commit v2 on v1

v2 whole, which is shorter than its diff:
```python
import functools

import jax
import jax.numpy as jnp
from jax import lax
from jax.experimental import pallas as pl
from jax.experimental.pallas import tpu as pltpu
from jax.sharding import PartitionSpec as P

MOMENTUM = 0.9
MESH = pl.DeviceIdType.MESH
BIT = {"c": 1, "x": 2, "y": 4, "a": 8, "b": 16}

bf, f32 = jnp.bfloat16, jnp.float32
TN = (((0,), (0,)), ((), ()))
NT = (((1,), (1,)), ((), ()))
def dot(a, b): return jnp.dot(a, b, preferred_element_type=f32)
def gelu_tanh(v): return jax.nn.gelu(v, approximate=True)

def back_sum_kernel(layers, scale, nu, tr, tw, lags, orders, *refs):
    (x, y, h_last, p_all, w_up, w_dn, gs, c_state, c_low, wup, wdn, w_s, g, acc, fin, rb0, rb1, rb2, rb3, rb4, c_s, c_r, rs_s, rs_r, ag_s, ag_r, d_s, d_r, st_s) = refs
    K = c_s.shape[0]
    NS, NF = acc.shape[0], fin.shape[0]
    l0, lrs, lag_, ld = lags
    me = lax.axis_index("data")
    bit = {d: lax.rem(me // BIT[d], 2) for d in BIT}
    peer = {d: me + BIT[d] * (1 - 2 * bit[d]) for d in BIT}
    bar = pltpu.get_barrier_semaphore()
    for d in "cxyab":
        pl.semaphore_signal(bar, inc=1, device_id=(peer[d],), device_id_type=MESH)
    pl.semaphore_wait(bar, 5)
    half = tr // 2
    rbs = [None, rb1, rb2, rb3, rb4]
    base, size = [], [half >> s for s in range(5)]
    for k, od in enumerate(orders):
        b = [k * half]
        for s, d in enumerate(od):
            b.append(b[-1] + size[s + 1] * bit[d])
        base.append(b)
    give = [[base[k][s] + size[s + 1] * (1 - bit[d]) for s, d in enumerate(od)] for k, od in enumerate(orders)]
    o = [0, l0]
    for s in range(4): o.append(o[-1] + lrs[s])
    for s in range(4): o.append(o[-1] + lag_[s])
    o.append(o[-1] + ld)
    assert NS >= o[5] and NF >= o[10] - o[1]
    AL = min(16, half // 16)
    def rows(off, n):
        return pl.ds(pl.multiple_of(off, AL), n)
    def own(u): return lax.rem(u // 8, 2), lax.rem(u, 8)
    def out(u): return nu - 8 - 8 * (u // 8) + lax.rem(u, 8)
    def cp_c(u):
        return pltpu.make_async_remote_copy(src_ref=g.at[(*own(u), 1 - bit["c"])], dst_ref=rb0.at[lax.rem(u, K)],
            send_sem=c_s.at[lax.rem(u, K)], recv_sem=c_r.at[lax.rem(u, K)], device_id=(peer["c"],), device_id_type=MESH)
    def cp_rs(u, k, s):
        return pltpu.make_async_remote_copy(src_ref=acc.at[lax.rem(u, NS), rows(give[k][s - 1], size[s])], dst_ref=rbs[s].at[k, lax.rem(u, K)],
            send_sem=rs_s.at[s - 1, k, lax.rem(u, K)], recv_sem=rs_r.at[s - 1, k, lax.rem(u, K)],
            device_id=(peer[orders[k][s - 1]],), device_id_type=MESH)
    def cp_ag(u, k, s):
        sl = fin.at[lax.rem(u, NF), rows(base[k][s], size[s])]
        return pltpu.make_async_remote_copy(src_ref=sl, dst_ref=sl, send_sem=ag_s.at[s - 1, k, lax.rem(u, K)], recv_sem=ag_r.at[s - 1, k, lax.rem(u, K)],
            device_id=(peer[orders[k][s - 1]],), device_id_type=MESH)
    def cp_d(u):
        return pltpu.make_async_remote_copy(src_ref=fin.at[lax.rem(u, NF)], dst_ref=gs.at[out(u), bit["c"]],
            send_sem=d_s.at[lax.rem(u, K)], recv_sem=d_r.at[lax.rem(u, K)], device_id=(peer["c"],), device_id_type=MESH)
    def cp_st(u):
        return pltpu.make_async_copy(fin.at[lax.rem(u, NF)], gs.at[out(u), bit["c"]], st_s.at[lax.rem(u, K)])
    def add_c(u):
        sl = lax.rem(u, NS)
        so, uo = own(u)
        for h in range(4):
            r = slice(h * tr // 4, (h + 1) * tr // 4)
            acc[sl, r] = (g[so, uo, bit["c"], r].astype(f32) + rb0[lax.rem(u, K), r].astype(f32)).astype(bf)
    def add_rs(u, k, s):
        sl = lax.rem(u, NS)
        r = rows(base[k][s], size[s])
        buf, so = (fin, lax.rem(u, NF)) if s == 4 else (acc, sl)
        buf[so, r] = (acc[sl, r].astype(jnp.float32) + rbs[s][k, lax.rem(u, K)].astype(jnp.float32)).astype(jnp.bfloat16)

    def tick(t, _):
        def ev(e, f):
            u = t - o[e]
            @pl.when(jnp.logical_and(u >= 0, u < nu))
            def _():
                f(u)
        def e10(u):
            cp_d(u).wait(); cp_st(u).wait()
        def e9(u):
            for k in range(2): cp_ag(u, k, 1).wait()
            cp_d(u).start(); cp_st(u).start()
        def mk_ag(s):
            def f(u):
                for k in range(2): cp_ag(u, k, s).wait()
                for k in range(2): cp_ag(u, k, s - 1).start()
            return f
        def e5(u):
            for k in range(2):
                cp_rs(u, k, 4).wait(); add_rs(u, k, 4)
            for k in range(2): cp_ag(u, k, 4).start()
        def mk_rs(s):
            def f(u):
                for k in range(2):
                    cp_rs(u, k, s - 1).wait(); add_rs(u, k, s - 1)
                for k in range(2): cp_rs(u, k, s).start()
            return f
        def e1(u):
            cp_c(u).wait(); add_c(u)
            for k in range(2): cp_rs(u, k, 1).start()
        def e0(u):
            cp_c(u).start()
        ev(10, e10); ev(9, e9)
        for e, s in ((8, 2), (7, 3), (6, 4)): ev(e, mk_ag(s))
        ev(5, e5)
        for e in (4, 3, 2): ev(e, mk_rs(e))
        ev(1, e1); ev(0, e0)
        return 0
    def cp_w(step, k):
        sl = lax.rem(step, 2)
        src, dst = ((w_up, wup), (w_dn, wdn))[k]
        return pltpu.make_async_copy(src.at[layers - 1 - step], dst.at[sl], w_s.at[k, sl])
    n = w_up.shape[2] // 4
    d2 = h_last.shape[1] // 2
    def chunk(step, q):
        sl = lax.rem(step, 2)
        @pl.when(jnp.logical_and(q == 0, step <= layers))
        def _():
            c_low[...] = c_state[...].astype(bf)
        @pl.when(jnp.logical_and(q == 0, step < layers))
        def _():
            for k in range(2): cp_w(step, k).wait()
        @pl.when(jnp.logical_and(q == 0, step < layers - 1))
        def _():
            for k in range(2): cp_w(step + 1, k).start()
        @pl.when(step < layers)
        def _():
            cols = pl.ds(pl.multiple_of(q * n, n), n)
            pin = p_all[layers - 1 - step]
            wu = wup[sl, :, cols].astype(bf)
            act, back = jax.vjp(gelu_tanh, dot(pin, wu))
            ac = lax.dot_general(c_low[...], wdn[sl, cols, :].astype(bf), NT, preferred_element_type=f32)
            pre = back(ac)[0].astype(bf)
            gd = lax.dot_general(act.astype(bf), c_low[...], TN, preferred_element_type=f32).astype(bf)
            gu = lax.dot_general(pin, pre, TN, preferred_element_type=f32).astype(bf)
            for t in range(2):
                g[sl, q, t] = gu[:, t * d2:(t + 1) * d2]
                g[sl, 4 + 2 * (q // 2) + t, lax.rem(q, 2)] = gd[:, t * d2:(t + 1) * d2]
            c_state[...] += lax.dot_general(pre, wu, NT, preferred_element_type=f32)
        @pl.when(step == layers)
        def _():
            for r in range(2):
                xs = x[:, pl.ds(pl.multiple_of((2 * q + r) * tr, tr), tr)]
                gi = lax.dot_general(xs, c_low[...], TN, preferred_element_type=f32).astype(bf)
                for t in range(2):
                    g[sl, 2 * q + t, r] = gi[:, t * d2:(t + 1) * d2]
    for k in range(2): cp_w(0, k).start()
    c_state[...] = (h_last[...] - y[...].astype(f32)) / scale
    def block(b, _):
        lax.fori_loop(2 * b - 8, 2 * b - 6, tick, 0)
        chunk(b // 4, lax.rem(b, 4))
        return 0
    lax.fori_loop(0, 4 + (nu + o[10] + 1) // 2, block, 0)

def backward_sum(scale, x, y, h_last, p_all, w_up, w_down, lags=(1, (3, 3, 3, 3), (3, 3, 3, 3), 1), orders=("xayb", "yaxb"), cid=0):
    layers, d, ff = w_up.shape
    nu, tr, tw = 8 * (layers + 1), 512, d // 2
    l0, lrs, lag_, ld = lags
    K = 2 * max(l0, ld, *lrs, *lag_)
    NS = l0 + sum(lrs)
    NF = sum(lrs) + sum(lag_) + ld
    half = tr // 2
    vm = pl.BlockSpec(memory_space=pltpu.VMEM)
    hb = pl.BlockSpec(memory_space=pl.ANY)
    return pl.pallas_call(
        functools.partial(back_sum_kernel, layers, scale, nu, tr, tw, lags, orders),
        out_shape=jax.ShapeDtypeStruct((nu, 2, tr, tw), bf),
        in_specs=[vm, vm, vm, vm, hb, hb],
        out_specs=hb,
        scratch_shapes=[pltpu.VMEM(h_last.shape, f32), pltpu.VMEM(h_last.shape, bf), pltpu.VMEM((2, d, ff), f32), pltpu.VMEM((2, ff, d), f32),
                        pltpu.SemaphoreType.DMA((2, 2)), pltpu.VMEM((2, 8, 2, tr, tw), bf),
                        pltpu.VMEM((NS, tr, tw), bf), pltpu.VMEM((NF, tr, tw), bf), pltpu.VMEM((K, tr, tw), bf)]
        + [pltpu.VMEM((2, K, half >> s, tw), bf) for s in range(1, 5)]
        + [pltpu.SemaphoreType.DMA((K,))] * 2 + [pltpu.SemaphoreType.DMA((4, 2, K))] * 4 + [pltpu.SemaphoreType.DMA((K,))] * 3,
        compiler_params=pltpu.CompilerParams(collective_id=cid, has_side_effects=True, vmem_limit_bytes=62 * 2**20),
        name="backward_sum",
    )(x, y, h_last, p_all, w_up, w_down)

def fwd_kernel(layers, x, w_in, w_up, w_down, p_out, h_out, h):
    i = pl.program_id(0)
    @pl.when(i < 4)
    def _():
        kq = x.shape[1]
        part = dot(x[...], w_in[...].astype(bf))
        @pl.when(i == 0)
        def _(): h[...] = part
        @pl.when(i > 0)
        def _(): h[...] += part
    @pl.when(i >= 4)
    def _():
        p = h[...].astype(bf)
        p_out[0] = p
        n = w_up.shape[2] // 4
        for q in range(4):
            c = slice(q * n, (q + 1) * n)
            u = dot(p, w_up[0, :, c].astype(bf))
            a = gelu_tanh(u).astype(bf)
            h[...] += dot(a, w_down[0, c, :].astype(bf))
    @pl.when(i == layers + 3)
    def _(): h_out[...] = h[...]

def forward(x, w_in, w_up, w_down):
    rows, e = x.shape
    layers, d, ff = w_up.shape
    lay = lambda i: jnp.maximum(i - 4, 0)
    return pl.pallas_call(
        functools.partial(fwd_kernel, layers), grid=(layers + 4,),
        out_shape=[jax.ShapeDtypeStruct((layers, rows, d), bf), jax.ShapeDtypeStruct((rows, d), f32)],
        in_specs=[pl.BlockSpec((rows, e // 4), lambda i: (0, jnp.minimum(i, 3))), pl.BlockSpec((e // 4, d), lambda i: (jnp.minimum(i, 3), 0)),
                  pl.BlockSpec((1, d, ff), lambda i: (lay(i), 0, 0)), pl.BlockSpec((1, ff, d), lambda i: (lay(i), 0, 0))],
        out_specs=[pl.BlockSpec((1, rows, d), lambda i: (lay(i), 0, 0)), pl.BlockSpec((rows, d), lambda i: (0, 0))],
        scratch_shapes=[pltpu.VMEM((rows, d), f32)],
        compiler_params=pltpu.CompilerParams(vmem_limit_bytes=60 * 2**20), name="forward",
    )(x, w_in, w_up, w_down)

def upd_kernel(layers, eta, mu, x, y, g, w_in, w_up, w_down, m_in, m_up, m_down,
               nw_in, nw_up, nw_down, nm_in, nm_up, nm_down, loss, h_out, h, p, a):
    i = pl.program_id(0)
    d = h.shape[1]
    d2 = d // 2
    v = i - 4
    r = lax.rem(jnp.maximum(v, 0), 4)
    def upd(w, m, nw, nm, u, t, ix):
        nmv = mu * m[ix] + g[u, t].astype(f32)
        nm[ix] = nmv
        nwv = w[ix] - eta * nmv
        nw[ix] = nwv
        return nwv.astype(bf)
    @pl.when(i < 4)
    def _():
        for j in range(2):
            cols = slice(j * d2, (j + 1) * d2)
            tot = None
            for t in range(2):
                s = slice(512 * t, 512 * (t + 1))
                q = dot(x[:, s], upd(w_in, m_in, nw_in, nm_in, j, t, (s, cols)))
                tot = q if tot is None else tot + q
            @pl.when(i == 0)
            def _(): h[:, cols] = tot
            @pl.when(i > 0)
            def _(): h[:, cols] += tot
    @pl.when(jnp.logical_and(v >= 0, r == 0))
    def _(): p[...] = h[...].astype(bf)
    @pl.when(jnp.logical_and(v >= 0, r < 2))
    def _():
        for j in range(2):
            for t in range(2):
                s = slice(512 * j + d2 * t, 512 * j + d2 * (t + 1))
                wl = upd(w_up, m_up, nw_up, nm_up, j, t, (0, slice(None), s))
                a[r, :, s] = gelu_tanh(dot(p[...], wl)).astype(bf)
    @pl.when(jnp.logical_and(v >= 0, r >= 2))
    def _():
        for j in range(2):
            cols = slice(j * d2, (j + 1) * d2)
            tot = None
            for t in range(2):
                s = slice(512 * t, 512 * (t + 1))
                q = dot(a[r - 2, :, s], upd(w_down, m_down, nw_down, nm_down, j, t, (0, s, cols)))
                tot = q if tot is None else tot + q
            h[:, cols] += tot
    @pl.when(i == 4 * layers + 3)
    def _():
        h_out[...] = h[...]
        e = h[...] - y[...].astype(f32)
        loss[...] = jnp.sum(e * e, axis=1, keepdims=True) / (2 * d)

def update(eta, mu, x, y, g, w_in, w_up, w_down, m_in, m_up, m_down):
    rows, e = x.shape
    layers, d, ff = w_up.shape
    nu = 8 * (layers + 1)
    q4 = lambda i: jnp.maximum(i - 4, 0)
    s_in = pl.BlockSpec((1024, d), lambda i: (jnp.minimum(i, 3), 0))
    s_up = pl.BlockSpec((1, d, 1024), lambda i: (q4(i) // 4, 0, jnp.minimum(lax.rem(q4(i), 4), 1)))
    s_dn = pl.BlockSpec((1, 1024, d), lambda i: (q4(i) // 4, jnp.maximum(lax.rem(q4(i), 4) - 2, 0), 0))
    x_spec = pl.BlockSpec((rows, 1024), lambda i: (0, jnp.minimum(i, 3)))
    full = pl.BlockSpec((rows, d), lambda i: (0, 0))
    o = [jax.ShapeDtypeStruct(t.shape, f32) for t in (w_in, w_up, w_down, m_in, m_up, m_down)]
    o += [jax.ShapeDtypeStruct((rows, 1), f32), jax.ShapeDtypeStruct((rows, d), f32)]
    return pl.pallas_call(
        functools.partial(upd_kernel, layers, eta, mu), grid=(nu // 2,), out_shape=o,
        in_specs=[x_spec, full, pl.BlockSpec((2, 2, 512, d // 2), lambda i: (i, 0, 0, 0)), s_in, s_up, s_dn, s_in, s_up, s_dn],
        out_specs=[s_in, s_up, s_dn, s_in, s_up, s_dn, pl.BlockSpec((rows, 1), lambda i: (0, 0)), full],
        scratch_shapes=[pltpu.VMEM((rows, d), f32), pltpu.VMEM((rows, d), bf), pltpu.VMEM((2, rows, 1024), bf)],
        compiler_params=pltpu.CompilerParams(vmem_limit_bytes=63 * 2**20), name="update",
    )(x, y, g, w_in, w_up, w_down, m_in, m_up, m_down)


def solution(mesh):
    group_size = mesh.shape["data"]

    def device_steps(w_in, w_up, w_down, mom_in, mom_up, mom_down, x_now, y_now, x_next, y_next):
        local_rows, model_width = y_now.shape
        step_size = 4.0 * model_width / (w_up.shape[2] * (w_up.shape[0] + 1))
        p_all, h_last = forward(x_now, w_in, w_up, w_down)
        total = backward_sum(float(local_rows * group_size * model_width), x_now, y_now, h_last, p_all, w_up, w_down)
        out = update(step_size, MOMENTUM, x_next, y_next, total, w_in, w_up, w_down, mom_in, mom_up, mom_down)
        return (*out[:6], out[6][:, 0], out[7])

    row_spec = P("data", None)
    return jax.shard_map(
        device_steps,
        mesh=mesh,
        in_specs=(P(),) * 6 + (row_spec,) * 4,
        out_specs=(P(),) * 6 + (P("data"), row_spec),
        check_vma=False,
    )
```

time: 705 us -> 619 us (0.88)
  Pallas kernels: 701 us -> 616 us
    pallas_call x3 -> x2, Pallas kernels: 659 us -> 574 us  [the longest x1 408 us: backward_sum(): pl.pallas_call(functools.partial(back_sum_kernel, layers, scale, nu, tr,...]
where the time goes in v2:
time: 619 us; the launch traced here: 618 us
  Pallas kernels  616 us (100%)
    pallas_call x1, Pallas kernels, backward_sum(): pl.pallas_call(functools.partial(back_sum_kernel, layers, scale, nu, tr,...  408 us
    pallas_call x1, Pallas kernels, update(): pl.pallas_call(functools.partial(upd_kernel, layers, eta, mu), grid=(nu /...  166 us
    pallas_call x1, Pallas kernels, forward(): pl.pallas_call(functools.partial(fwd_kernel, layers), grid=(layers + 4,),...  42.1 us

profile of v2, /device:TPU:0, one launch (start us, length us, event | category | flops | bytes accessed | tf_op | source)
XLA Modules:
  0.0 618.2 jit_solution(6483216716349699614)
XLA Ops:
  0.6 42.1 %forward.1 = (bf16[12,256,512]{2,1,0:T(8,128)(2,1)}, f32[256,512]{1,0:T(8,128)}) custom-call(bf16[256,4096]{1,0:T(8,128)(2,1)} %refs_0_.1, f32[4096,512]{1,0:T(8,128)} %w_in.3, f32[12,512,2048]{2,1,0:T(8,128)} %w_up.3, f32[12,2048,512]{2,1,0:T(8,128)} %w_down.3), custom_call_target="tpu_custom_call" | custom-call | tf_op jit(solution)/shard_map/forward/pallas_call | solution.py:213
  42.7 408.2 %backward_sum.1.g = bf16[104,2,512,256]{3,2,1,0:T(8,128)(2,1)} custom-call(bf16[256,4096]{1,0:T(8,128)(2,1)} %refs_0_.1, bf16[256,512]{1,0:T(8,128)(2,1)} %refs_1_.1, f32[256,512]{1,0:T(8,128)} %get-tuple-element.18.refs_2_, bf16[12,256,512]{2,1,0:T(8,128)(2,1)} %get-tuple-element.19.refs_3_, f32[12,512,2048]{2,1,0:T(8,128)} %w_up.3, f32[12,2048,512]{2,1,0:T(8,128)} %w_down.3), custom_call_target="tpu_custom_call" | custom-call | tf_op jit(solution)/shard_map/backward_sum/pallas_call | solution.py:172
  450.9 165.7 %update.1 = (f32[4096,512]{1,0:T(8,128)}, f32[12,512,2048]{2,1,0:T(8,128)}, f32[12,2048,512]{2,1,0:T(8,128)}, f32[4096,512]{1,0:T(8,128)}, f32[12,512,2048]{2,1,...) custom-call(bf16[256,4096]{1,0:T(8,128)(2,1)} %x.3, bf16[256,512]{1,0:T(8,128)(2,1)} %y.1, ...), custom_call_target="tpu_custom_call" | custom-call | tf_op jit(solution)/shard_map/update/pallas_call | solution.py:286
  616.6 1.6 reduce

commit v3 on v2

--- a/solution.py
+++ b/solution.py
@@ -17,101 +17,144 @@
 def dot(a, b): return jnp.dot(a, b, preferred_element_type=f32)
 def gelu_tanh(v): return jax.nn.gelu(v, approximate=True)
 
-def back_sum_kernel(layers, scale, nu, tr, tw, lags, orders, *refs):
-    (x, y, h_last, p_all, w_up, w_dn, gs, c_state, c_low, wup, wdn, w_s, g, acc, fin, rb0, rb1, rb2, rb3, rb4, c_s, c_r, rs_s, rs_r, ag_s, ag_r, d_s, d_r, st_s) = refs
-    K = c_s.shape[0]
-    NS, NF = acc.shape[0], fin.shape[0]
-    l0, lrs, lag_, ld = lags
+def back_sum_kernel(layers, scale, nu, tr, tw, lags, *refs):
+    (x, y, h_last, p_all, w_up, w_dn, gs, c_state, c_low, wup, wdn, w_s, g, acc, fin, rb0, rb1, rb3, rzu, rzd,
+     c_s, c_r, b_s, b_r, s_s, s_r, zr_s, zr_r, za_s, za_r, t_s, t_r, v_s, v_r, d_s, d_r, st_s) = refs
+    K, KZ, NS, NF = c_s.shape[0], rzu.shape[1], acc.shape[0], fin.shape[0]
+    l0, lx, lz, ly, ld = lags
     me = lax.axis_index("data")
-    bit = {d: lax.rem(me // BIT[d], 2) for d in BIT}
-    peer = {d: me + BIT[d] * (1 - 2 * bit[d]) for d in BIT}
+    bit = {"c": lax.rem(me, 2), "x": lax.rem(me // 2, 2), "y": lax.rem(me // 4, 2)}
+    peer = {d: me + w * (1 - 2 * bit[d]) for d, w in (("c", 1), ("x", 2), ("y", 4))}
+    z = me // 8
     bar = pltpu.get_barrier_semaphore()
-    for d in "cxyab":
-        pl.semaphore_signal(bar, inc=1, device_id=(peer[d],), device_id_type=MESH)
-    pl.semaphore_wait(bar, 5)
-    half = tr // 2
-    rbs = [None, rb1, rb2, rb3, rb4]
-    base, size = [], [half >> s for s in range(5)]
-    for k, od in enumerate(orders):
-        b = [k * half]
-        for s, d in enumerate(od):
-            b.append(b[-1] + size[s + 1] * bit[d])
-        base.append(b)
-    give = [[base[k][s] + size[s + 1] * (1 - bit[d]) for s, d in enumerate(od)] for k, od in enumerate(orders)]
-    o = [0, l0]
-    for s in range(4): o.append(o[-1] + lrs[s])
-    for s in range(4): o.append(o[-1] + lag_[s])
-    o.append(o[-1] + ld)
-    assert NS >= o[5] and NF >= o[10] - o[1]
-    AL = min(16, half // 16)
+    def greet(dev):
+        pl.semaphore_signal(bar, inc=1, device_id=(dev,), device_id_type=MESH)
+    for d in "cxy":
+        greet(peer[d])
+    pl.when(z < 3)(lambda: greet(me + 8))
+    pl.when(z > 0)(lambda: greet(me - 8))
+    pl.semaphore_wait(bar, 3 + jnp.minimum(z, 1) + jnp.minimum(3 - z, 1))
+    half, big, ch = tr // 2, tr // 4, tr // 16
+    small = ch // 2
+    D1, D2 = "xy", "yx"
+    base0 = [0, half]
+    base1 = [base0[k] + big * bit[D1[k]] for k in range(2)]
+    give1 = [base0[k] + big * (1 - bit[D1[k]]) for k in range(2)]
+    base3 = [base1[k] + ch * z + small * bit[D2[k]] for k in range(2)]
+    give3 = [base1[k] + ch * z + small * (1 - bit[D2[k]]) for k in range(2)]
+    o1 = l0
+    o2 = o1 + lx
+    o3 = o2 + 3 * lz
+    o4 = o3 + ly
+    o5 = o4 + ly
+    o6 = o5 + 3 * lz
+    o7 = o6 + lx
+    o8 = o7 + ld
+    assert NS >= o4 and NF >= o8 - o1
     def rows(off, n):
-        return pl.ds(pl.multiple_of(off, AL), n)
+        return pl.ds(pl.multiple_of(off, min(16, small)), n)
+    def remote(src, dst, ss, rs, dev):
+        return pltpu.make_async_remote_copy(src_ref=src, dst_ref=dst, send_sem=ss, recv_sem=rs, device_id=(dev,), device_id_type=MESH)
+    def ix(u): return lax.rem(u, K)
+    def iz(u): return lax.rem(u, KZ)
+    def accr(u, off, n): return acc.at[lax.rem(u, NS), rows(off, n)]
+    def finr(u, off, n): return fin.at[lax.rem(u, NF), rows(off, n)]
     def own(u): return lax.rem(u // 8, 2), lax.rem(u, 8)
     def out(u): return nu - 8 - 8 * (u // 8) + lax.rem(u, 8)
     def cp_c(u):
-        return pltpu.make_async_remote_copy(src_ref=g.at[(*own(u), 1 - bit["c"])], dst_ref=rb0.at[lax.rem(u, K)],
-            send_sem=c_s.at[lax.rem(u, K)], recv_sem=c_r.at[lax.rem(u, K)], device_id=(peer["c"],), device_id_type=MESH)
-    def cp_rs(u, k, s):
-        return pltpu.make_async_remote_copy(src_ref=acc.at[lax.rem(u, NS), rows(give[k][s - 1], size[s])], dst_ref=rbs[s].at[k, lax.rem(u, K)],
-            send_sem=rs_s.at[s - 1, k, lax.rem(u, K)], recv_sem=rs_r.at[s - 1, k, lax.rem(u, K)],
-            device_id=(peer[orders[k][s - 1]],), device_id_type=MESH)
-    def cp_ag(u, k, s):
-        sl = fin.at[lax.rem(u, NF), rows(base[k][s], size[s])]
-        return pltpu.make_async_remote_copy(src_ref=sl, dst_ref=sl, send_sem=ag_s.at[s - 1, k, lax.rem(u, K)], recv_sem=ag_r.at[s - 1, k, lax.rem(u, K)],
-            device_id=(peer[orders[k][s - 1]],), device_id_type=MESH)
+        return remote(g.at[(*own(u), 1 - bit["c"])], rb0.at[ix(u)], c_s.at[ix(u)], c_r.at[ix(u)], peer["c"])
+    def cp_b(u, k):
+        return remote(accr(u, give1[k], big), rb1.at[k, ix(u)], b_s.at[k, ix(u)], b_r.at[k, ix(u)], peer[D1[k]])
+    def cp_s(u, k):
+        return remote(accr(u, give3[k], small), rb3.at[k, ix(u)], s_s.at[k, ix(u)], s_r.at[k, ix(u)], peer[D2[k]])
+    def cp_v(u, k):
+        r = finr(u, base3[k], small)
+        return remote(r, r, v_s.at[k, ix(u)], v_r.at[k, ix(u)], peer[D2[k]])
+    def cp_t(u, k):
+        r = finr(u, base1[k], big)
+        return remote(r, r, t_s.at[k, ix(u)], t_r.at[k, ix(u)], peer[D1[k]])
     def cp_d(u):
-        return pltpu.make_async_remote_copy(src_ref=fin.at[lax.rem(u, NF)], dst_ref=gs.at[out(u), bit["c"]],
-            send_sem=d_s.at[lax.rem(u, K)], recv_sem=d_r.at[lax.rem(u, K)], device_id=(peer["c"],), device_id_type=MESH)
+        return remote(fin.at[lax.rem(u, NF)], gs.at[out(u), bit["c"]], d_s.at[ix(u)], d_r.at[ix(u)], peer["c"])
     def cp_st(u):
-        return pltpu.make_async_copy(fin.at[lax.rem(u, NF)], gs.at[out(u), bit["c"]], st_s.at[lax.rem(u, K)])
-    def add_c(u):
-        sl = lax.rem(u, NS)
-        so, uo = own(u)
-        for h in range(4):
-            r = slice(h * tr // 4, (h + 1) * tr // 4)
-            acc[sl, r] = (g[so, uo, bit["c"], r].astype(f32) + rb0[lax.rem(u, K), r].astype(f32)).astype(bf)
-    def add_rs(u, k, s):
-        sl = lax.rem(u, NS)
-        r = rows(base[k][s], size[s])
-        buf, so = (fin, lax.rem(u, NF)) if s == 4 else (acc, sl)
-        buf[so, r] = (acc[sl, r].astype(jnp.float32) + rbs[s][k, lax.rem(u, K)].astype(jnp.float32)).astype(jnp.bfloat16)
-
+        return pltpu.make_async_copy(fin.at[lax.rem(u, NF)], gs.at[out(u), bit["c"]], st_s.at[ix(u)])
+    def cp_zr(u, k, side, f, n):
+        buf = (rzu, rzd)[side].at[k, iz(u), pl.ds(0, n * ch)]
+        return remote(accr(u, base1[k] + ch * f, n * ch), buf, zr_s.at[side, k, iz(u)], zr_r.at[side, k, iz(u)], me + (8, -8)[side])
+    def cp_za(u, k, side, f, n):
+        r = finr(u, base1[k] + ch * f, n * ch)
+        return remote(r, r, za_s.at[side, k, iz(u)], za_r.at[side, k, iz(u)], me + (8, -8)[side])
+    snd_r = [lambda q: (q + 1, 3 - q), lambda q: (0, q)]
+    rcv_r = [lambda q: (q, 4 - q), lambda q: (0, q + 1)]
+    snd_a = [lambda q: (0, q + 1), lambda q: (q, 4 - q)]
+    rcv_a = [lambda q: (0, q), lambda q: (q + 1, 3 - q)]
+    senders, takers = [(0, 1, 2), (1, 2, 3)], [(1, 2, 3), (0, 1, 2)]
+    def add(dst, slot, r, a, b):
+        dst[slot, r] = (a.astype(f32) + b.astype(f32)).astype(bf)
     def tick(t, _):
-        def ev(e, f):
-            u = t - o[e]
-            @pl.when(jnp.logical_and(u >= 0, u < nu))
-            def _():
-                f(u)
-        def e10(u):
+        def ev(off, f):
+            u = t - off
+            pl.when(jnp.logical_and(u >= 0, u < nu))(lambda: f(u))
+        def pair(cp, what):
+            def f(u):
+                for k in range(2): getattr(cp(u, k), what)()
+            return f
+        def line(o, cp, snd, rcv, take):
+            at = [o + z * lz, o + (3 - z) * lz]
+            for side in range(2):
+                for q in senders[side]:
+                    def sent(u, side=side, q=q):
+                        for k in range(2): cp(u, k, side, *snd[side](q)).wait_send()
+                    pl.when(z == q)(lambda: ev(at[side] + lz, sent))
+                for q in takers[side]:
+                    def got(u, side=side, q=q):
+                        for k in range(2):
+                            cp(u, k, side, *rcv[side](q)).wait_recv()
+                            take(u, k, side, *rcv[side](q))
+                    pl.when(z == q)(lambda: ev(at[side], got))
+            for side in range(2):
+                for q in senders[side]:
+                    def send(u, side=side, q=q):
+                        for k in range(2): cp(u, k, side, *snd[side](q)).start()
+                    pl.when(z == q)(lambda: ev(at[side], send))
+        def take_r(u, k, side, f, n):
+            r = rows(base1[k] + ch * f, n * ch)
+            add(acc, lax.rem(u, NS), r, acc[lax.rem(u, NS), r], (rzu, rzd)[side][k, iz(u), 0:n * ch])
+        def take_a(u, k, side, f, n):
+            pass
+        def e8(u):
             cp_d(u).wait(); cp_st(u).wait()
-        def e9(u):
-            for k in range(2): cp_ag(u, k, 1).wait()
+        def e7(u):
+            pair(cp_t, "wait")(u)
             cp_d(u).start(); cp_st(u).start()
-        def mk_ag(s):
-            def f(u):
-                for k in range(2): cp_ag(u, k, s).wait()
-                for k in range(2): cp_ag(u, k, s - 1).start()
-            return f
-        def e5(u):
+        def e4(u):
             for k in range(2):
-                cp_rs(u, k, 4).wait(); add_rs(u, k, 4)
-            for k in range(2): cp_ag(u, k, 4).start()
-        def mk_rs(s):
-            def f(u):
-                for k in range(2):
-                    cp_rs(u, k, s - 1).wait(); add_rs(u, k, s - 1)
-                for k in range(2): cp_rs(u, k, s).start()
-            return f
+                cp_s(u, k).wait()
+                r = rows(base3[k], small)
+                add(fin, lax.rem(u, NF), r, acc[lax.rem(u, NS), r], rb3[k, ix(u)])
+            pair(cp_v, "start")(u)
+        def e2(u):
+            for k in range(2):
+                cp_b(u, k).wait()
+                r = rows(base1[k], big)
+                add(acc, lax.rem(u, NS), r, acc[lax.rem(u, NS), r], rb1[k, ix(u)])
         def e1(u):
-            cp_c(u).wait(); add_c(u)
-            for k in range(2): cp_rs(u, k, 1).start()
-        def e0(u):
-            cp_c(u).start()
-        ev(10, e10); ev(9, e9)
-        for e, s in ((8, 2), (7, 3), (6, 4)): ev(e, mk_ag(s))
-        ev(5, e5)
-        for e in (4, 3, 2): ev(e, mk_rs(e))
-        ev(1, e1); ev(0, e0)
+            cp_c(u).wait()
+            so, uo = own(u)
+            for h in range(4):
+                r = slice(h * big, (h + 1) * big)
+                add(acc, lax.rem(u, NS), r, g[so, uo, bit["c"], r], rb0[ix(u), r])
+            pair(cp_b, "start")(u)
+        ev(o8, e8)
+        ev(o7, e7)
+        ev(o5, pair(cp_v, "wait"))
+        line(o5, cp_za, snd_a, rcv_a, take_a)
+        ev(o6, pair(cp_t, "start"))
+        ev(o4, e4)
+        ev(o2, e2)
+        line(o2, cp_zr, snd_r, rcv_r, take_r)
+        ev(o3, pair(cp_s, "start"))
+        ev(o1, e1)
+        ev(0, lambda u: cp_c(u).start())
         return 0
     def cp_w(step, k):
         sl = lax.rem(step, 2)
@@ -157,28 +200,30 @@
         lax.fori_loop(2 * b - 8, 2 * b - 6, tick, 0)
         chunk(b // 4, lax.rem(b, 4))
         return 0
-    lax.fori_loop(0, 4 + (nu + o[10] + 1) // 2, block, 0)
-
-def backward_sum(scale, x, y, h_last, p_all, w_up, w_down, lags=(1, (3, 3, 3, 3), (3, 3, 3, 3), 1), orders=("xayb", "yaxb"), cid=0):
+    lax.fori_loop(0, 4 + (nu + o8 + 1) // 2, block, 0)
+
+def backward_sum(scale, x, y, h_last, p_all, w_up, w_down, lags=(1, 2, 2, 2, 1), cid=0):
     layers, d, ff = w_up.shape
     nu, tr, tw = 8 * (layers + 1), 512, d // 2
-    l0, lrs, lag_, ld = lags
-    K = 2 * max(l0, ld, *lrs, *lag_)
-    NS = l0 + sum(lrs)
-    NF = sum(lrs) + sum(lag_) + ld
-    half = tr // 2
+    l0, lx, lz, ly, ld = lags
+    K = 2 * max(lags)
+    KZ = 3 * max(lags)
+    NS = l0 + lx + 3 * lz + ly
+    NF = 2 * lx + 6 * lz + 2 * ly + ld
     vm = pl.BlockSpec(memory_space=pltpu.VMEM)
     hb = pl.BlockSpec(memory_space=pl.ANY)
+    sem = pltpu.SemaphoreType.DMA
     return pl.pallas_call(
-        functools.partial(back_sum_kernel, layers, scale, nu, tr, tw, lags, orders),
+        functools.partial(back_sum_kernel, layers, scale, nu, tr, tw, lags),
         out_shape=jax.ShapeDtypeStruct((nu, 2, tr, tw), bf),
         in_specs=[vm, vm, vm, vm, hb, hb],
         out_specs=hb,
         scratch_shapes=[pltpu.VMEM(h_last.shape, f32), pltpu.VMEM(h_last.shape, bf), pltpu.VMEM((2, d, ff), f32), pltpu.VMEM((2, ff, d), f32),
-                        pltpu.SemaphoreType.DMA((2, 2)), pltpu.VMEM((2, 8, 2, tr, tw), bf),
-                        pltpu.VMEM((NS, tr, tw), bf), pltpu.VMEM((NF, tr, tw), bf), pltpu.VMEM((K, tr, tw), bf)]
-        + [pltpu.VMEM((2, K, half >> s, tw), bf) for s in range(1, 5)]
-        + [pltpu.SemaphoreType.DMA((K,))] * 2 + [pltpu.SemaphoreType.DMA((4, 2, K))] * 4 + [pltpu.SemaphoreType.DMA((K,))] * 3,
+                        sem((2, 2)), pltpu.VMEM((2, 8, 2, tr, tw), bf),
+                        pltpu.VMEM((NS, tr, tw), bf), pltpu.VMEM((NF, tr, tw), bf), pltpu.VMEM((K, tr, tw), bf),
+                        pltpu.VMEM((2, K, tr // 4, tw), bf), pltpu.VMEM((2, K, tr // 32, tw), bf),
+                        pltpu.VMEM((2, KZ, 3 * tr // 16, tw), bf), pltpu.VMEM((2, KZ, 3 * tr // 16, tw), bf)]
+        + [sem((K,))] * 2 + [sem((2, K))] * 4 + [sem((2, 2, KZ))] * 4 + [sem((2, K))] * 4 + [sem((K,))] * 3,
         compiler_params=pltpu.CompilerParams(collective_id=cid, has_side_effects=True, vmem_limit_bytes=62 * 2**20),
         name="backward_sum",
     )(x, y, h_last, p_all, w_up, w_down)

time: 619 us -> 584 us (0.943)
  Pallas kernels: 616 us -> 582 us
    pallas_call x1, Pallas kernels: 408 us -> 374 us  [backward_sum(): pl.pallas_call(functools.partial(back_sum_kernel, layers, scale, nu, tr,...]
where the time goes in v3:
time: 584 us
  Pallas kernels  582 us (100%)
    pallas_call x1, Pallas kernels, backward_sum(): pl.pallas_call(functools.partial(back_sum_kernel, layers, scale, nu, tr,...  374 us
    pallas_call x1, Pallas kernels, update(): pl.pallas_call(functools.partial(upd_kernel, layers, eta, mu), grid=(nu /...  166 us
    pallas_call x1, Pallas kernels, forward(): pl.pallas_call(functools.partial(fwd_kernel, layers), grid=(layers + 4,),...  42.1 us

profile of v3, /device:TPU:0, one launch (start us, length us, event | category | flops | bytes accessed | tf_op | source)
XLA Modules:
  0.0 583.9 jit_solution(17908094682960890389)
XLA Ops:
  0.6 42.1 %forward.1 = (bf16[12,256,512]{2,1,0:T(8,128)(2,1)}, f32[256,512]{1,0:T(8,128)}) custom-call(bf16[256,4096]{1,0:T(8,128)(2,1)} %refs_0_.1, f32[4096,512]{1,0:T(8,128)} %w_in.3, f32[12,512,2048]{2,1,0:T(8,128)} %w_up.3, f32[12,2048,512]{2,1,0:T(8,128)} %w_down.3), custom_call_target="tpu_custom_call" | custom-call | tf_op jit(solution)/shard_map/forward/pallas_call | solution.py:258
  42.7 374.0 %backward_sum.1.g = bf16[104,2,512,256]{3,2,1,0:T(8,128)(2,1)} custom-call(bf16[256,4096]{1,0:T(8,128)(2,1)} %refs_0_.1, bf16[256,512]{1,0:T(8,128)(2,1)} %refs_1_.1, f32[256,512]{1,0:T(8,128)} %get-tuple-element.18.refs_2_, bf16[12,256,512]{2,1,0:T(8,128)(2,1)} %get-tuple-element.19.refs_3_, f32[12,512,2048]{2,1,0:T(8,128)} %w_up.3, f32[12,2048,512]{2,1,0:T(8,128)} %w_down.3), custom_call_target="tpu_custom_call" | custom-call | tf_op jit(solution)/shard_map/backward_sum/pallas_call | solution.py:216
  416.7 165.6 %update.1 = (f32[4096,512]{1,0:T(8,128)}, f32[12,512,2048]{2,1,0:T(8,128)}, f32[12,2048,512]{2,1,0:T(8,128)}, f32[4096,512]{1,0:T(8,128)}, f32[12,512,2048]{2,1,...) custom-call(bf16[256,4096]{1,0:T(8,128)(2,1)} %x.3, bf16[256,512]{1,0:T(8,128)(2,1)} %y.1, ...), custom_call_target="tpu_custom_call" | custom-call | tf_op jit(solution)/shard_map/update/pallas_call | solution.py:331
  582.3 1.6 reduce

commit v4 on v3

v4 whole, which is shorter than its diff:
```python
import functools

import jax
import jax.numpy as jnp
from jax import lax
from jax.experimental import pallas as pl
from jax.experimental.pallas import tpu as pltpu
from jax.sharding import PartitionSpec as P

MOMENTUM = 0.9
MESH = pl.DeviceIdType.MESH
BIT = {"c": 1, "x": 2, "y": 4, "a": 8, "b": 16}

bf, f32 = jnp.bfloat16, jnp.float32
TN = (((0,), (0,)), ((), ()))
NT = (((1,), (1,)), ((), ()))
def dot(a, b): return jnp.dot(a, b, preferred_element_type=f32)
def gelu_tanh(v): return jax.nn.gelu(v, approximate=True)

def grad_sum_kernel(layers, scale, nu, tr, tw, lags, *refs):
    (x_hbm, y, w_in, w_up, w_dn, gs, x, p_all, c_state, c_low, wup, wdn, w_s, x_s, g, acc, fin, rb0, rb1, rb3, rzu, rzd,
     c_s, c_r, b_s, b_r, s_s, s_r, zr_s, zr_r, za_s, za_r, t_s, t_r, v_s, v_r, d_s, d_r, st_s) = refs
    K, KZ, NS, NF = c_s.shape[0], rzu.shape[1], acc.shape[0], fin.shape[0]
    l0, lx, lz, ly, ld = lags
    me = lax.axis_index("data")
    bit = {"c": lax.rem(me, 2), "x": lax.rem(me // 2, 2), "y": lax.rem(me // 4, 2)}
    peer = {d: me + w * (1 - 2 * bit[d]) for d, w in (("c", 1), ("x", 2), ("y", 4))}
    z = me // 8
    bar = pltpu.get_barrier_semaphore()
    def greet(dev):
        pl.semaphore_signal(bar, inc=1, device_id=(dev,), device_id_type=MESH)
    for d in "cxy":
        greet(peer[d])
    pl.when(z < 3)(lambda: greet(me + 8))
    pl.when(z > 0)(lambda: greet(me - 8))
    half, big, ch = tr // 2, tr // 4, tr // 16
    small = ch // 2
    D1, D2 = "xy", "yx"
    base0 = [0, half]
    base1 = [base0[k] + big * bit[D1[k]] for k in range(2)]
    give1 = [base0[k] + big * (1 - bit[D1[k]]) for k in range(2)]
    base3 = [base1[k] + ch * z + small * bit[D2[k]] for k in range(2)]
    give3 = [base1[k] + ch * z + small * (1 - bit[D2[k]]) for k in range(2)]
    o1 = l0
    o2 = o1 + lx
    o3 = o2 + 3 * lz
    o4 = o3 + ly
    o5 = o4 + ly
    o6 = o5 + 3 * lz
    o7 = o6 + lx
    o8 = o7 + ld
    assert NS >= o4 and NF >= o8 - o1
    def rows(off, n):
        return pl.ds(pl.multiple_of(off, min(16, small)), n)
    def remote(src, dst, ss, rs, dev):
        return pltpu.make_async_remote_copy(src_ref=src, dst_ref=dst, send_sem=ss, recv_sem=rs, device_id=(dev,), device_id_type=MESH)
    def ix(u): return lax.rem(u, K)
    def iz(u): return lax.rem(u, KZ)
    def accr(u, off, n): return acc.at[lax.rem(u, NS), rows(off, n)]
    def finr(u, off, n): return fin.at[lax.rem(u, NF), rows(off, n)]
    def own(u): return lax.rem(u // 8, 2), lax.rem(u, 8)
    def out(u): return nu - 8 - 8 * (u // 8) + lax.rem(u, 8)
    def cp_c(u):
        return remote(g.at[(*own(u), 1 - bit["c"])], rb0.at[ix(u)], c_s.at[ix(u)], c_r.at[ix(u)], peer["c"])
    def cp_b(u, k):
        return remote(accr(u, give1[k], big), rb1.at[k, ix(u)], b_s.at[k, ix(u)], b_r.at[k, ix(u)], peer[D1[k]])
    def cp_s(u, k):
        return remote(accr(u, give3[k], small), rb3.at[k, ix(u)], s_s.at[k, ix(u)], s_r.at[k, ix(u)], peer[D2[k]])
    def cp_v(u, k):
        r = finr(u, base3[k], small)
        return remote(r, r, v_s.at[k, ix(u)], v_r.at[k, ix(u)], peer[D2[k]])
    def cp_t(u, k):
        r = finr(u, base1[k], big)
        return remote(r, r, t_s.at[k, ix(u)], t_r.at[k, ix(u)], peer[D1[k]])
    def cp_d(u):
        return remote(fin.at[lax.rem(u, NF)], gs.at[out(u), bit["c"]], d_s.at[ix(u)], d_r.at[ix(u)], peer["c"])
    def cp_st(u):
        return pltpu.make_async_copy(fin.at[lax.rem(u, NF)], gs.at[out(u), bit["c"]], st_s.at[ix(u)])
    def cp_zr(u, k, side, f, n):
        buf = (rzu, rzd)[side].at[k, iz(u), pl.ds(0, n * ch)]
        return remote(accr(u, base1[k] + ch * f, n * ch), buf, zr_s.at[side, k, iz(u)], zr_r.at[side, k, iz(u)], me + (8, -8)[side])
    def cp_za(u, k, side, f, n):
        r = finr(u, base1[k] + ch * f, n * ch)
        return remote(r, r, za_s.at[side, k, iz(u)], za_r.at[side, k, iz(u)], me + (8, -8)[side])
    snd_r = [lambda q: (q + 1, 3 - q), lambda q: (0, q)]
    rcv_r = [lambda q: (q, 4 - q), lambda q: (0, q + 1)]
    snd_a = [lambda q: (0, q + 1), lambda q: (q, 4 - q)]
    rcv_a = [lambda q: (0, q), lambda q: (q + 1, 3 - q)]
    senders, takers = [(0, 1, 2), (1, 2, 3)], [(1, 2, 3), (0, 1, 2)]
    def add(dst, slot, r, a, b):
        dst[slot, r] = (a.astype(f32) + b.astype(f32)).astype(bf)
    def tick(t, _):
        def ev(off, f):
            u = t - off
            pl.when(jnp.logical_and(u >= 0, u < nu))(lambda: f(u))
        def pair(cp, what):
            def f(u):
                for k in range(2): getattr(cp(u, k), what)()
            return f
        def line(o, cp, snd, rcv, take):
            at = [o + z * lz, o + (3 - z) * lz]
            for side in range(2):
                for q in senders[side]:
                    def sent(u, side=side, q=q):
                        for k in range(2): cp(u, k, side, *snd[side](q)).wait_send()
                    pl.when(z == q)(lambda: ev(at[side] + lz, sent))
                for q in takers[side]:
                    def got(u, side=side, q=q):
                        for k in range(2):
                            cp(u, k, side, *rcv[side](q)).wait_recv()
                            take(u, k, side, *rcv[side](q))
                    pl.when(z == q)(lambda: ev(at[side], got))
            for side in range(2):
                for q in senders[side]:
                    def send(u, side=side, q=q):
                        for k in range(2): cp(u, k, side, *snd[side](q)).start()
                    pl.when(z == q)(lambda: ev(at[side], send))
        def take_r(u, k, side, f, n):
            r = rows(base1[k] + ch * f, n * ch)
            add(acc, lax.rem(u, NS), r, acc[lax.rem(u, NS), r], (rzu, rzd)[side][k, iz(u), 0:n * ch])
        def take_a(u, k, side, f, n):
            pass
        def e8(u):
            cp_d(u).wait(); cp_st(u).wait()
        def e7(u):
            pair(cp_t, "wait")(u)
            cp_d(u).start(); cp_st(u).start()
        def e4(u):
            for k in range(2):
                cp_s(u, k).wait()
                r = rows(base3[k], small)
                add(fin, lax.rem(u, NF), r, acc[lax.rem(u, NS), r], rb3[k, ix(u)])
            pair(cp_v, "start")(u)
        def e2(u):
            for k in range(2):
                cp_b(u, k).wait()
                r = rows(base1[k], big)
                add(acc, lax.rem(u, NS), r, acc[lax.rem(u, NS), r], rb1[k, ix(u)])
        def e1(u):
            cp_c(u).wait()
            so, uo = own(u)
            for h in range(4):
                r = slice(h * big, (h + 1) * big)
                add(acc, lax.rem(u, NS), r, g[so, uo, bit["c"], r], rb0[ix(u), r])
            pair(cp_b, "start")(u)
        ev(o8, e8)
        ev(o7, e7)
        ev(o5, pair(cp_v, "wait"))
        line(o5, cp_za, snd_a, rcv_a, take_a)
        ev(o6, pair(cp_t, "start"))
        ev(o4, e4)
        ev(o2, e2)
        line(o2, cp_zr, snd_r, rcv_r, take_r)
        ev(o3, pair(cp_s, "start"))
        ev(o1, e1)
        ev(0, lambda u: cp_c(u).start())
        return 0
    d, ff = w_up.shape[1:]
    def cp_w(layer, k):
        sl = lax.rem(layer, 2)
        src, dst = ((w_up, wup), (w_dn, wdn))[k]
        return pltpu.make_async_copy(src.at[layer], dst.at[sl], w_s.at[k, sl])
    e4 = w_in.shape[0] // 4
    cp_x = pltpu.make_async_copy(x_hbm, x, x_s.at[4])
    cp_in = [pltpu.make_async_copy(w_in.at[pl.ds(i * e4, e4)], wdn.at[i // 2, pl.ds((i % 2) * e4, e4)], x_s.at[i]) for i in range(4)]
    cp_x.start()
    for c in cp_in: c.start()
    for l in range(2): cp_w(l, 0).start()
    cp_x.wait()
    h = c_state
    for i in range(4):
        cp_in[i].wait()
        part = dot(x[:, i * e4:(i + 1) * e4], wdn[i // 2, (i % 2) * e4:(i % 2 + 1) * e4].astype(bf))
        h[...] = part if i == 0 else h[...] + part
        if i % 2 == 1: cp_w(i // 2, 1).start()
    n = ff // 4
    def layer_fwd(l, _):
        sl = lax.rem(l, 2)
        pin = h[...].astype(bf)
        p_all[l] = pin
        tot = h[...]
        cp_w(l, 0).wait()
        acts = [gelu_tanh(dot(pin, wup[sl, :, q * n:(q + 1) * n].astype(bf))).astype(bf) for q in range(4)]
        cp_w(l, 1).wait()
        for q in range(4):
            tot = tot + dot(acts[q], wdn[sl, q * n:(q + 1) * n].astype(bf))
        h[...] = tot
        @pl.when(l < layers - 2)
        def _():
            for k in range(2): cp_w(l + 2, k).start()
        return 0
    lax.fori_loop(0, layers, layer_fwd, 0)
    c_state[...] = (h[...] - y[...].astype(f32)) / scale
    pl.semaphore_wait(bar, 3 + jnp.minimum(z, 1) + jnp.minimum(3 - z, 1))
    d2 = d // 2
    def chunk(step, q):
        gl = lax.rem(step, 2)
        layer = layers - 1 - step
        sl = lax.rem(layer, 2)
        @pl.when(jnp.logical_and(q == 0, step <= layers))
        def _():
            c_low[...] = c_state[...].astype(bf)
        @pl.when(jnp.logical_and(q == 0, jnp.logical_and(step >= 2, step < layers)))
        def _():
            for k in range(2): cp_w(layer, k).wait()
        @pl.when(jnp.logical_and(q == 0, jnp.logical_and(step >= 1, step < layers - 1)))
        def _():
            for k in range(2): cp_w(layer - 1, k).start()
        @pl.when(step < layers)
        def _():
            cols = pl.ds(pl.multiple_of(q * n, n), n)
            pin = p_all[layer]
            wu = wup[sl, :, cols].astype(bf)
            act, back = jax.vjp(gelu_tanh, dot(pin, wu))
            ac = lax.dot_general(c_low[...], wdn[sl, cols, :].astype(bf), NT, preferred_element_type=f32)
            pre = back(ac)[0].astype(bf)
            gd = lax.dot_general(act.astype(bf), c_low[...], TN, preferred_element_type=f32).astype(bf)
            gu = lax.dot_general(pin, pre, TN, preferred_element_type=f32).astype(bf)
            for t in range(2):
                g[gl, 4 * (q // 2) + lax.rem(q, 2), t] = gu[:, t * d2:(t + 1) * d2]
                g[gl, 4 * (q // 2) + 2 + t, lax.rem(q, 2)] = gd[:, t * d2:(t + 1) * d2]
            c_state[...] += lax.dot_general(pre, wu, NT, preferred_element_type=f32)
        @pl.when(step == layers)
        def _():
            for r in range(2):
                xs = x[:, pl.ds(pl.multiple_of((2 * q + r) * tr, tr), tr)]
                gi = lax.dot_general(xs, c_low[...], TN, preferred_element_type=f32).astype(bf)
                for t in range(2):
                    g[gl, 2 * q + t, r] = gi[:, t * d2:(t + 1) * d2]
    def block(b, _):
        lax.fori_loop(2 * b - 4, 2 * b - 2, tick, 0)
        chunk(b // 4, lax.rem(b, 4))
        return 0
    lax.fori_loop(0, 2 + (nu + o8 + 1) // 2, block, 0)

def gradient_sum(scale, x, y, w_in, w_up, w_down, lags=(1, 2, 2, 2, 1), cid=0):
    layers, d, ff = w_up.shape
    rows = x.shape[0]
    nu, tr, tw = 8 * (layers + 1), 512, d // 2
    l0, lx, lz, ly, ld = lags
    K = 2 * max(lags)
    KZ = 3 * max(lags)
    NS = l0 + lx + 3 * lz + ly
    NF = 2 * lx + 6 * lz + 2 * ly + ld
    vm = pl.BlockSpec(memory_space=pltpu.VMEM)
    hb = pl.BlockSpec(memory_space=pl.ANY)
    sem = pltpu.SemaphoreType.DMA
    return pl.pallas_call(
        functools.partial(grad_sum_kernel, layers, scale, nu, tr, tw, lags),
        out_shape=jax.ShapeDtypeStruct((nu, 2, tr, tw), bf),
        in_specs=[hb, vm, hb, hb, hb],
        out_specs=hb,
        scratch_shapes=[pltpu.VMEM(x.shape, bf), pltpu.VMEM((layers, rows, d), bf), pltpu.VMEM((rows, d), f32), pltpu.VMEM((rows, d), bf),
                        pltpu.VMEM((2, d, ff), f32), pltpu.VMEM((2, ff, d), f32), sem((2, 2)), sem((5,)), pltpu.VMEM((2, 8, 2, tr, tw), bf),
                        pltpu.VMEM((NS, tr, tw), bf), pltpu.VMEM((NF, tr, tw), bf), pltpu.VMEM((K, tr, tw), bf),
                        pltpu.VMEM((2, K, tr // 4, tw), bf), pltpu.VMEM((2, K, tr // 32, tw), bf),
                        pltpu.VMEM((2, KZ, 3 * tr // 16, tw), bf), pltpu.VMEM((2, KZ, 3 * tr // 16, tw), bf)]
        + [sem((K,))] * 2 + [sem((2, K))] * 4 + [sem((2, 2, KZ))] * 4 + [sem((2, K))] * 4 + [sem((K,))] * 3,
        compiler_params=pltpu.CompilerParams(collective_id=cid, has_side_effects=True, vmem_limit_bytes=62 * 2**20),
        name="gradient_sum",
    )(x, y, w_in, w_up, w_down)


SLOTS = 4
def upd_kernel(layers, eta, mu, x, y, gs, w_in, w_up, w_dn, m_in, m_up, m_dn,
               nw_in, nw_up, nw_dn, nm_in, nm_up, nm_dn, loss, h_out, wu, mu_, wd, md, g, h, p, a, ld_s, st_s):
    d, ff = w_up.shape[1:]
    d2, hf = d // 2, ff // 2
    steps = 4 + 2 * layers
    def where(s):
        v = jnp.maximum(s - 4, 0)
        return v // 2, lax.rem(v, 2)
    def moves(s, kind, put):
        sl = lax.rem(s, SLOTS)
        if kind == 0:
            at = pl.ds(pl.multiple_of(s * hf, hf), hf)
            arr = [((w_in, nw_in)[put].at[at], wd.at[sl]), ((m_in, nm_in)[put].at[at], md.at[sl])]
            gsrc, gdst = gs.at[pl.ds(2 * s, 2)], g.at[sl, pl.ds(0, 2)]
        else:
            l, j = where(s)
            at = pl.ds(pl.multiple_of(j * hf, hf), hf)
            arr = [((w_up, nw_up)[put].at[l, :, at], wu.at[sl]), ((m_up, nm_up)[put].at[l, :, at], mu_.at[sl]),
                   ((w_dn, nw_dn)[put].at[l, at], wd.at[sl]), ((m_dn, nm_dn)[put].at[l, at], md.at[sl])]
            gsrc, gdst = gs.at[pl.ds(8 + 8 * l + 4 * j, 4)], g.at[sl]
        if put:
            return [pltpu.make_async_copy(v, hb, st_s.at[sl, i]) for i, (hb, v) in enumerate(arr)]
        return [pltpu.make_async_copy(hb, v, ld_s.at[sl, i]) for i, (hb, v) in enumerate(arr)] + [pltpu.make_async_copy(gsrc, gdst, ld_s.at[sl, 4])]
    def go(s, put, what):
        @pl.when(jnp.logical_and(s >= 0, s < 4))
        def _():
            for c in moves(s, 0, put): getattr(c, what)()
        @pl.when(jnp.logical_and(s >= 4, s < steps))
        def _():
            for c in moves(s, 1, put): getattr(c, what)()
    for s in range(SLOTS - 1): go(jnp.int32(s), 0, "start")
    h[...] = jnp.zeros_like(h)
    def step(s, _):
        sl = lax.rem(s, SLOTS)
        go(s, 0, "wait")
        def upd(w, m, u, t, ix):
            nm = mu * m[(sl, *ix)] + g[sl, u, t].astype(f32)
            m[(sl, *ix)] = nm
            nw = w[(sl, *ix)] - eta * nm
            w[(sl, *ix)] = nw
            return nw.astype(bf)
        def down(lhs, u0):
            for j in range(2):
                cols = slice(j * d2, (j + 1) * d2)
                tot = h[:, cols]
                for t in range(2):
                    r = slice(t * hf // 2, (t + 1) * hf // 2)
                    tot = tot + dot(lhs(r), upd(wd, md, u0 + j, t, (r, cols)))
                h[:, cols] = tot
        @pl.when(s < 4)
        def _():
            xs = x[:, pl.ds(pl.multiple_of(s * hf, hf), hf)]
            down(lambda r: xs[:, r], 0)
        @pl.when(s >= 4)
        def _():
            @pl.when(lax.rem(s, 2) == 0)
            def _(): p[...] = h[...].astype(bf)
            for j in range(2):
                for t in range(2):
                    cols = slice(hf // 2 * j + d2 * t, hf // 2 * j + d2 * (t + 1))
                    a[:, cols] = gelu_tanh(dot(p[...], upd(wu, mu_, j, t, (slice(None), cols)))).astype(bf)
            down(lambda r: a[:, r], 2)
        go(s, 1, "start")
        go(s - 1, 1, "wait")
        go(s + SLOTS - 1, 0, "start")
        return 0
    lax.fori_loop(0, steps, step, 0)
    h_out[...] = h[...]
    e = h[...] - y[...].astype(f32)
    loss[...] = jnp.sum(e * e, axis=1) / (2 * d)
    go(jnp.int32(steps - 1), 1, "wait")

def update(eta, mu, x, y, g, w_in, w_up, w_down, m_in, m_up, m_down):
    rows = x.shape[0]
    layers, d, ff = w_up.shape
    vm = pl.BlockSpec(memory_space=pltpu.VMEM)
    hb = pl.BlockSpec(memory_space=pl.ANY)
    o = [jax.ShapeDtypeStruct(t.shape, f32) for t in (w_in, w_up, w_down, m_in, m_up, m_down)]
    o += [jax.ShapeDtypeStruct((rows,), f32), jax.ShapeDtypeStruct((rows, d), f32)]
    tile = [pltpu.VMEM((SLOTS, d, ff // 2), f32)] * 2 + [pltpu.VMEM((SLOTS, ff // 2, d), f32)] * 2
    return pl.pallas_call(
        functools.partial(upd_kernel, layers, eta, mu), out_shape=o,
        in_specs=[vm, vm] + [hb] * 7, out_specs=[hb] * 6 + [vm, vm],
        scratch_shapes=tile + [pltpu.VMEM((SLOTS, 4, 2, 512, d // 2), bf), pltpu.VMEM((rows, d), f32), pltpu.VMEM((rows, d), bf),
                               pltpu.VMEM((rows, ff // 2), bf), pltpu.SemaphoreType.DMA((SLOTS, 5)), pltpu.SemaphoreType.DMA((SLOTS, 4))],
        compiler_params=pltpu.CompilerParams(vmem_limit_bytes=63 * 2**20), name="update",
    )(x, y, g, w_in, w_up, w_down, m_in, m_up, m_down)


def solution(mesh):
    group_size = mesh.shape["data"]

    def device_steps(w_in, w_up, w_down, mom_in, mom_up, mom_down, x_now, y_now, x_next, y_next):
        local_rows, model_width = y_now.shape
        step_size = 4.0 * model_width / (w_up.shape[2] * (w_up.shape[0] + 1))
        total = gradient_sum(float(local_rows * group_size * model_width), x_now, y_now, w_in, w_up, w_down)
        out = update(step_size, MOMENTUM, x_next, y_next, total, w_in, w_up, w_down, mom_in, mom_up, mom_down)
        return tuple(out)

    row_spec = P("data", None)
    return jax.shard_map(
        device_steps,
        mesh=mesh,
        in_specs=(P(),) * 6 + (row_spec,) * 4,
        out_specs=(P(),) * 6 + (P("data"), row_spec),
        check_vma=False,
    )
```

time: 584 us -> 556 us (0.952)
  Pallas kernels: 582 us -> 555 us
    pallas_call x3 -> x2, Pallas kernels: 582 us -> 555 us  [the longest x1 399 us: gradient_sum(): pl.pallas_call(functools.partial(grad_sum_kernel, layers, scale, nu, tr,...]
where the time goes in v4:
time: 556 us
  Pallas kernels  555 us (100%)
    pallas_call x1, Pallas kernels, gradient_sum(): pl.pallas_call(functools.partial(grad_sum_kernel, layers, scale, nu, tr,...  399 us
    pallas_call x1, Pallas kernels, update(): pl.pallas_call(functools.partial(upd_kernel, layers, eta, mu), out_shape=...  157 us

profile of v4, /device:TPU:0, one launch (start us, length us, event | category | flops | bytes accessed | tf_op | source)
XLA Modules:
  0.0 556.1 jit_solution(10678983010834225821)
XLA Ops:
  0.6 398.6 %gradient_sum.1.gs = bf16[104,2,512,256]{3,2,1,0:T(8,128)(2,1)} custom-call(bf16[256,4096]{1,0:T(8,128)(2,1)} %refs_0_.1, bf16[256,512]{1,0:T(8,128)(2,1)} %refs_1_.1, f32[4096,512]{1,0:T(8,128)} %w_in.1, f32[12,512,2048]{2,1,0:T(8,128)} %w_up.1, f32[12,2048,512]{2,1,0:T(8,128)} %w_dn.1), custom_call_target="tpu_custom_call" | custom-call | tf_op jit(solution)/shard_map/gradient_sum/pallas_call | solution.py:248
  399.2 156.9 %update.1 = (f32[4096,512]{1,0:T(8,128)}, f32[12,512,2048]{2,1,0:T(8,128)}, f32[12,2048,512]{2,1,0:T(8,128)}, f32[4096,512]{1,0:T(8,128)}, f32[12,512,2048]{2,1,...) custom-call(bf16[256,4096]{1,0:T(8,128)(2,1)} %x.1, bf16[256,512]{1,0:T(8,128)(2,1)} %y.1, ...), custom_call_target="tpu_custom_call" | custom-call | tf_op jit(solution)/shard_map/update/pallas_call | solution.py:345

commit v5 on v4

v5 whole, which is shorter than its diff:
```python
import functools

import jax
import jax.numpy as jnp
from jax import lax
from jax.experimental import pallas as pl
from jax.experimental.pallas import tpu as pltpu
from jax.sharding import PartitionSpec as P

MOMENTUM = 0.9
MESH = pl.DeviceIdType.MESH
BIT = {"c": 1, "x": 2, "y": 4, "a": 8, "b": 16}

bf, f32 = jnp.bfloat16, jnp.float32
TN = (((0,), (0,)), ((), ()))
NT = (((1,), (1,)), ((), ()))
def dot(a, b): return jnp.dot(a, b, preferred_element_type=f32)
def gelu_tanh(v): return jax.nn.gelu(v, approximate=True)

HOPS = {"mid": (0, "z", 1), "late": (0, 1, "z"), "early": ("z", 0, 1)}

def plan(types, tr, tw, K, KZ):
    sem, out = pltpu.SemaphoreType.DMA, []
    for ty in types:
        size = tr // 2
        for s, hop in enumerate(HOPS[ty]):
            if hop == "z":
                size //= 4
                out += [((ty, s, b), pltpu.VMEM((2, KZ, 3 * size, tw), bf)) for b in ("up", "down")]
                out += [((ty, s, b), sem((2, 2, KZ))) for b in ("rs", "rr", "as", "ar")]
            else:
                size //= 2
                out += [((ty, s, "buf"), pltpu.VMEM((2, K, size, tw), bf))]
                out += [((ty, s, b), sem((2, K))) for b in ("rs", "rr", "as", "ar")]
    return out

def grad_sum_kernel(layers, scale, nu, part, tr, tw, lags, kinds, names, *refs):
    (x_hbm, y, w_in, w_up, w_dn, gs, own_a, own_b, oth_a, oth_b, x, p_all, c_state, c_low, wup, wdn, w_s, x_s, g, acc, fin, rb0,
     c_s, c_r, d_s, d_r, st_s, h_s, h_r, hs_s) = refs[:30]
    mem = dict(zip(names, refs[30:]))
    types = sorted({n[0] for n in names})
    K, NS, NF = c_s.shape[0], acc.shape[0], fin.shape[0]
    KZ = [mem[n].shape[1] for n in names if n[2] == "up"][0]
    l0, lp, lz, ld = lags
    me = lax.axis_index("data")
    bit = {"c": lax.rem(me, 2), "x": lax.rem(me // 2, 2), "y": lax.rem(me // 4, 2)}
    peer = {d: me + w * (1 - 2 * bit[d]) for d, w in (("c", 1), ("x", 2), ("y", 4))}
    z = me // 8
    bar = pltpu.get_barrier_semaphore()
    def greet(dev):
        pl.semaphore_signal(bar, inc=1, device_id=(dev,), device_id_type=MESH)
    for d in "cxy":
        greet(peer[d])
    pl.when(z < 3)(lambda: greet(me + 8))
    pl.when(z > 0)(lambda: greet(me - 8))
    half, big = tr // 2, tr // 4
    DIMS = ("xy", "yx")
    o1 = l0
    def offsets(ty):
        zl = lz[ty]
        o4 = o1 + 2 * lp + 3 * zl
        o7 = 2 * o4 - o1
        return zl, o4, o7, o7 + ld
    o8 = max(offsets(ty)[3] for ty in types)
    assert NS >= max(offsets(ty)[1] for ty in types) and NF >= o8 - o1
    def rows(off, n):
        return pl.ds(pl.multiple_of(off, 16), n)
    def remote(src, dst, ss, rs, dev):
        return pltpu.make_async_remote_copy(src_ref=src, dst_ref=dst, send_sem=ss, recv_sem=rs, device_id=(dev,), device_id_type=MESH)
    def ix(u): return lax.rem(u, K)
    def iz(u): return lax.rem(u, KZ)
    def accr(u, off, n): return acc.at[lax.rem(u, NS), rows(off, n)]
    def finr(u, off, n): return fin.at[lax.rem(u, NF), rows(off, n)]
    def own(u): return lax.rem(u // 8, 2), lax.rem(u, 8)
    def out(u): return nu - 8 - 8 * (u // 8) + lax.rem(u, 8)
    def out_p(u): return part - 8 - 8 * (u // 8) + lax.rem(u, 8)
    def cp_c(u):
        return remote(g.at[(*own(u), 1 - bit["c"])], rb0.at[ix(u)], c_s.at[ix(u)], c_r.at[ix(u)], peer["c"])
    def cp_d(u):
        return remote(fin.at[lax.rem(u, NF)], gs.at[out(u), bit["c"]], d_s.at[ix(u)], d_r.at[ix(u)], peer["c"])
    def cp_st(u):
        return pltpu.make_async_copy(fin.at[lax.rem(u, NF)], gs.at[out(u), bit["c"]], st_s.at[ix(u)])
    home = [k * half + big * bit[DIMS[k][0]] for k in range(2)]
    def cp_h(u, k):
        return remote(finr(u, home[k], big), (oth_a, oth_b)[k].at[out_p(u)], h_s.at[k, ix(u)], h_r.at[k, ix(u)], peer["c"])
    def cp_hs(u, k):
        return pltpu.make_async_copy(finr(u, home[k], big), (own_a, own_b)[k].at[out_p(u)], hs_s.at[k, ix(u)])
    def add(dst, slot, r, a, b):
        dst[slot, r] = (a.astype(f32) + b.astype(f32)).astype(bf)
    snd_r = [lambda q: (q + 1, 3 - q), lambda q: (0, q)]
    rcv_r = [lambda q: (q, 4 - q), lambda q: (0, q + 1)]
    snd_a = [lambda q: (0, q + 1), lambda q: (q, 4 - q)]
    rcv_a = [lambda q: (0, q), lambda q: (q + 1, 3 - q)]
    senders, takers = [(0, 1, 2), (1, 2, 3)], [(1, 2, 3), (0, 1, 2)]
    def tick(t, _):
        def ev(off, f, cond=None):
            u = t - off
            ok = jnp.logical_and(u >= 0, u < nu)
            if cond is not None: ok = jnp.logical_and(ok, cond(u))
            pl.when(ok)(lambda: f(u))
        def whole(u): return u >= part
        def left(u): return u < part
        def e8(u):
            cp_d(u).wait(); cp_st(u).wait()
        def e8p(u):
            for k in range(2):
                cp_h(u, k).wait(); cp_hs(u, k).wait()
        def e7(u):
            cp_d(u).start(); cp_st(u).start()
        def e6p(u):
            for k in range(2):
                cp_h(u, k).start(); cp_hs(u, k).start()
        def e1(u):
            cp_c(u).wait()
            so, uo = own(u)
            for q in range(4):
                r = slice(q * big, (q + 1) * big)
                add(acc, lax.rem(u, NS), r, g[so, uo, bit["c"], r], rb0[ix(u), r])
        def line(ty, s, base, ch, o, lz, cond, gather, what):
            bufs, names_ = (mem[ty, s, "up"], mem[ty, s, "down"]), ("as", "ar") if gather else ("rs", "rr")
            snd, rcv = (snd_a, rcv_a) if gather else (snd_r, rcv_r)
            at = [o + z * lz, o + (3 - z) * lz]
            def cp(u, k, side, f, n):
                ss, rs = (mem[ty, s, m].at[side, k, iz(u)] for m in names_)
                r = (finr if gather else accr)(u, base[k] + ch * f, n * ch)
                return remote(r, r if gather else bufs[side].at[k, iz(u), pl.ds(0, n * ch)], ss, rs, me + (8, -8)[side])
            for side in range(2):
                if what == "arrive":
                    for q in senders[side]:
                        def sent(u, side=side, q=q):
                            for k in range(2): cp(u, k, side, *snd[side](q)).wait_send()
                        pl.when(z == q)(lambda: ev(at[side] + lz, sent, cond))
                    for q in takers[side]:
                        def got(u, side=side, q=q):
                            f, n = rcv[side](q)
                            for k in range(2):
                                cp(u, k, side, f, n).wait_recv()
                                if not gather:
                                    r = rows(base[k] + ch * f, n * ch)
                                    add(acc, lax.rem(u, NS), r, acc[lax.rem(u, NS), r], bufs[side][k, iz(u), 0:n * ch])
                        pl.when(z == q)(lambda: ev(at[side], got, cond))
                else:
                    for q in senders[side]:
                        def send(u, side=side, q=q):
                            for k in range(2): cp(u, k, side, *snd[side](q)).start()
                        pl.when(z == q)(lambda: ev(at[side], send, cond))
        def flow(ty):
            zl, o4, o7, o8 = offsets(ty)
            mine = lambda u: kinds(u, ty)
            mine_whole = lambda u: jnp.logical_and(mine(u), whole(u))
            ev(o8, e8, mine_whole)
            if part: ev(o7, e8p, lambda u: jnp.logical_and(mine(u), left(u)))
            base, size, hops = [[0, half]], [half], []
            o = o1
            for s, hop in enumerate(HOPS[ty]):
                if hop == "z":
                    n = size[-1] // 4
                    nb = [b + n * z for b in base[-1]]
                    give, dim = None, None
                    lag = 3 * zl
                else:
                    n = size[-1] // 2
                    dim = [DIMS[k][hop] for k in range(2)]
                    nb = [base[-1][k] + n * bit[dim[k]] for k in range(2)]
                    give = [base[-1][k] + n * (1 - bit[dim[k]]) for k in range(2)]
                    lag = lp
                hops.append((s, hop, base[-1], nb, n, give, dim, o, o + lag))
                base.append(nb); size.append(n)
                o += lag
            last_base, last = base[-1], size[-1]
            def pair_cp(u, k, s, src, dst, pre, dev):
                return remote(src, dst, mem[ty, s, pre + "s"].at[k, ix(u)], mem[ty, s, pre + "r"].at[k, ix(u)], peer[dev])
            o = o7
            for i, (s, hop, b, nb, n, give, dim, _, _) in enumerate(hops):
                cond = mine_whole if i == 0 else mine
                if hop == "z":
                    line(ty, s, b, n, o - 3 * zl, zl, cond, True, "arrive")
                else:
                    def arrive(u, s=s, nb=nb, n=n, dim=dim):
                        for k in range(2): pair_cp(u, k, s, finr(u, nb[k], n), finr(u, nb[k], n), "a", dim[k]).wait()
                    ev(o, arrive, cond)
                if i == 0:
                    ev(o7, e7, mine_whole)
                else:
                    depart_g(*prev)
                    if i == 1 and part: ev(o, e6p, lambda u: jnp.logical_and(mine(u), left(u)))
                def depart_g(s, hop, b, nb, n, dim, o, cond):
                    if hop == "z":
                        line(ty, s, b, n, o, zl, cond, True, "depart")
                    else:
                        def go(u):
                            for k in range(2): pair_cp(u, k, s, finr(u, nb[k], n), finr(u, nb[k], n), "a", dim[k]).start()
                        ev(o, go, cond)
                o -= 3 * zl if hop == "z" else lp
                prev = (s, hop, b, nb, n, dim, o, cond)
            for i, (s, hop, b, nb, n, give, dim, oa, ob) in reversed(list(enumerate(hops))):
                if hop == "z":
                    line(ty, s, b, n, oa, zl, mine, False, "arrive")
                else:
                    def arrive(u, s=s, nb=nb, n=n, give=give, dim=dim):
                        for k in range(2):
                            pair_cp(u, k, s, accr(u, give[k], n), mem[ty, s, "buf"].at[k, ix(u)], "r", dim[k]).wait()
                            r = rows(nb[k], n)
                            add(acc, lax.rem(u, NS), r, acc[lax.rem(u, NS), r], mem[ty, s, "buf"][k, ix(u)])
                    ev(ob, arrive, mine)
                if i == len(hops) - 1:
                    def finish(u):
                        for k in range(2):
                            r = rows(last_base[k], last)
                            fin[lax.rem(u, NF), r] = acc[lax.rem(u, NS), r]
                    ev(o4, finish, mine)
                    depart_g(*prev)
                else:
                    depart_r(*prev_r)
                def depart_r(s, hop, b, n, give, dim, oa):
                    if hop == "z":
                        line(ty, s, b, n, oa, zl, mine, False, "depart")
                    else:
                        def go(u):
                            for k in range(2): pair_cp(u, k, s, accr(u, give[k], n), mem[ty, s, "buf"].at[k, ix(u)], "r", dim[k]).start()
                        ev(oa, go, mine)
                prev_r = (s, hop, b, n, give, dim, oa)
            return depart_r, prev_r
        firsts = [flow(ty) for ty in types]
        ev(o1, e1)
        for f, args in firsts: f(*args)
        ev(0, lambda u: cp_c(u).start())
        return 0
    d, ff = w_up.shape[1:]
    def cp_w(layer, k):
        sl = lax.rem(layer, 2)
        src, dst = ((w_up, wup), (w_dn, wdn))[k]
        return pltpu.make_async_copy(src.at[layer], dst.at[sl], w_s.at[k, sl])
    e4 = w_in.shape[0] // 4
    cp_x = pltpu.make_async_copy(x_hbm, x, x_s.at[4])
    cp_in = [pltpu.make_async_copy(w_in.at[pl.ds(i * e4, e4)], wdn.at[i // 2, pl.ds((i % 2) * e4, e4)], x_s.at[i]) for i in range(4)]
    cp_x.start()
    for c in cp_in: c.start()
    for l in range(2): cp_w(l, 0).start()
    cp_x.wait()
    h = c_state
    for i in range(4):
        cp_in[i].wait()
        piece = dot(x[:, i * e4:(i + 1) * e4], wdn[i // 2, (i % 2) * e4:(i % 2 + 1) * e4].astype(bf))
        h[...] = piece if i == 0 else h[...] + piece
        if i % 2 == 1: cp_w(i // 2, 1).start()
    n = ff // 4
    def layer_fwd(l, _):
        sl = lax.rem(l, 2)
        pin = h[...].astype(bf)
        p_all[l] = pin
        tot = h[...]
        cp_w(l, 0).wait()
        acts = [gelu_tanh(dot(pin, wup[sl, :, q * n:(q + 1) * n].astype(bf))).astype(bf) for q in range(4)]
        cp_w(l, 1).wait()
        for q in range(4):
            tot = tot + dot(acts[q], wdn[sl, q * n:(q + 1) * n].astype(bf))
        h[...] = tot
        @pl.when(l < layers - 2)
        def _():
            for k in range(2): cp_w(l + 2, k).start()
        return 0
    lax.fori_loop(0, layers, layer_fwd, 0)
    c_state[...] = (h[...] - y[...].astype(f32)) / scale
    pl.semaphore_wait(bar, 3 + jnp.minimum(z, 1) + jnp.minimum(3 - z, 1))
    d2 = d // 2
    def chunk(step, q):
        gl = lax.rem(step, 2)
        layer = layers - 1 - step
        sl = lax.rem(layer, 2)
        @pl.when(jnp.logical_and(q == 0, step <= layers))
        def _():
            c_low[...] = c_state[...].astype(bf)
        @pl.when(jnp.logical_and(q == 0, jnp.logical_and(step >= 2, step < layers)))
        def _():
            for k in range(2): cp_w(layer, k).wait()
        @pl.when(jnp.logical_and(q == 0, jnp.logical_and(step >= 1, step < layers - 1)))
        def _():
            for k in range(2): cp_w(layer - 1, k).start()
        @pl.when(step < layers)
        def _():
            cols = pl.ds(pl.multiple_of(q * n, n), n)
            pin = p_all[layer]
            wu = wup[sl, :, cols].astype(bf)
            act, back = jax.vjp(gelu_tanh, dot(pin, wu))
            ac = lax.dot_general(c_low[...], wdn[sl, cols, :].astype(bf), NT, preferred_element_type=f32)
            pre = back(ac)[0].astype(bf)
            gd = lax.dot_general(act.astype(bf), c_low[...], TN, preferred_element_type=f32).astype(bf)
            gu = lax.dot_general(pin, pre, TN, preferred_element_type=f32).astype(bf)
            for t in range(2):
                g[gl, 4 * (q // 2) + lax.rem(q, 2), t] = gu[:, t * d2:(t + 1) * d2]
                g[gl, 4 * (q // 2) + 2 + t, lax.rem(q, 2)] = gd[:, t * d2:(t + 1) * d2]
            c_state[...] += lax.dot_general(pre, wu, NT, preferred_element_type=f32)
        @pl.when(step == layers)
        def _():
            for r in range(2):
                xs = x[:, pl.ds(pl.multiple_of((2 * q + r) * tr, tr), tr)]
                gi = lax.dot_general(xs, c_low[...], TN, preferred_element_type=f32).astype(bf)
                for t in range(2):
                    g[gl, 2 * q + t, r] = gi[:, t * d2:(t + 1) * d2]
    def block(b, _):
        lax.fori_loop(2 * b - 4, 2 * b - 2, tick, 0)
        chunk(b // 4, lax.rem(b, 4))
        return 0
    lax.fori_loop(0, 2 + (nu + o8 + 1) // 2, block, 0)

def gradient_sum(scale, x, y, w_in, w_up, w_down, part, kinds, types, lags=(1, 2, {"mid": 2, "late": 2, "early": 4}, 1), cid=0, K=8, KZ=8, NS=16, NF=32):
    layers, d, ff = w_up.shape
    rows = x.shape[0]
    nu, tr, tw = 8 * (layers + 1), 512, d // 2
    l0, lp, lz, ld = lags
    vm = pl.BlockSpec(memory_space=pltpu.VMEM)
    hb = pl.BlockSpec(memory_space=pl.ANY)
    sem = pltpu.SemaphoreType.DMA
    hops = plan(types, tr, tw, K, KZ)
    left = jax.ShapeDtypeStruct((max(part, 8), tr // 4, tw), bf)
    return pl.pallas_call(
        functools.partial(grad_sum_kernel, layers, scale, nu, part, tr, tw, lags, kinds, [n for n, _ in hops]),
        out_shape=[jax.ShapeDtypeStruct((nu - part, 2, tr, tw), bf)] + [left] * 4,
        in_specs=[hb, vm, hb, hb, hb],
        out_specs=[hb] * 5,
        scratch_shapes=[pltpu.VMEM(x.shape, bf), pltpu.VMEM((layers, rows, d), bf), pltpu.VMEM((rows, d), f32), pltpu.VMEM((rows, d), bf),
                        pltpu.VMEM((2, d, ff), f32), pltpu.VMEM((2, ff, d), f32), sem((2, 2)), sem((5,)), pltpu.VMEM((2, 8, 2, tr, tw), bf),
                        pltpu.VMEM((NS, tr, tw), bf), pltpu.VMEM((NF, tr, tw), bf), pltpu.VMEM((K, tr, tw), bf)]
        + [sem((K,))] * 5 + [sem((2, K))] * 3 + [spec for _, spec in hops],
        compiler_params=pltpu.CompilerParams(collective_id=cid, has_side_effects=True, vmem_limit_bytes=63 * 2**20),
        name="gradient_sum",
    )(x, y, w_in, w_up, w_down)


SLOTS = 4
def upd_kernel(layers, lo, hi, eta, mu, *refs):
    scratch = refs[-11:]
    wu, mu_, wd, md, g, h, p, a, ld_s, st_s, g_s = scratch
    first, last = lo == 0, hi == layers
    if first:
        x, gs, w_in, w_up, w_dn, m_in, m_up, m_dn, nw_in, nw_up, nw_dn, nm_in, nm_up, nm_dn, h_out = refs[:-11]
    elif last:
        y, h_in, *pieces = refs[:10]
        w_up, w_dn, m_up, m_dn, _, _, _, _, nw_up, nw_dn, nm_up, nm_dn, loss, h_out = refs[10:-11]
    else:
        h_in, gs, w_up, w_dn, m_up, m_dn, _, _, _, _, nw_up, nw_dn, nm_up, nm_dn, h_out = refs[:-11]
    d, ff = w_up.shape[1:]
    d2, hf = d // 2, ff // 2
    ins = 4 if first else 0
    steps = ins + 2 * (hi - lo)
    def where(s):
        v = jnp.maximum(s - ins, 0)
        return lo + v // 2, lax.rem(v, 2)
    def moves(s, group, put):
        sl = lax.rem(s, SLOTS)
        if group == "in":
            at = pl.ds(pl.multiple_of(s * hf, hf), hf)
            arr = [((w_in, nw_in)[put].at[at], wd.at[sl]), ((m_in, nm_in)[put].at[at], md.at[sl])]
        else:
            l, j = where(s)
            at = pl.ds(pl.multiple_of(j * hf, hf), hf)
            if group == "up":
                arr = [((w_up, nw_up)[put].at[l, :, at], wu.at[sl]), ((m_up, nm_up)[put].at[l, :, at], mu_.at[sl])]
            else:
                arr = [((w_dn, nw_dn)[put].at[l, at], wd.at[sl]), ((m_dn, nm_dn)[put].at[l, at], md.at[sl])]
        o = 0 if group == "up" else 2
        sems = (ld_s, st_s)[put]
        return [pltpu.make_async_copy(*((v, hb) if put else (hb, v)), sems.at[sl, o + i]) for i, (hb, v) in enumerate(arr)]
    def grads(s, kind, what):
        sl = lax.rem(s, SLOTS)
        if kind == "in":
            c = pltpu.make_async_copy(gs.at[pl.ds(2 * s, 2)], g.at[sl, pl.ds(0, 2)], g_s.at[sl, 0])
            return getattr(c, what)()
        l, j = where(s)
        if not last:
            c = pltpu.make_async_copy(gs.at[pl.ds(8 + 8 * l + 4 * j, 4)], g.at[sl], g_s.at[sl, 0])
            return getattr(c, what)()
        me = lax.axis_index("data")
        c, q = lax.rem(me, 2), 128
        at = 8 * (l - lo) + 4 * j
        for k in range(2):
            b = lax.rem(me // (2, 4)[k], 2)
            for i in range(4):
                row = pl.multiple_of(256 * k + q * (b if i < 2 else 1 - b), q)
                half = c if i % 2 == 0 else 1 - c
                cp = pltpu.make_async_copy(pieces[4 * k + i].at[pl.ds(at, 4)], g.at[sl, :, half, pl.ds(row, q)], g_s.at[sl, 4 * k + i])
                getattr(cp, what)()
    def on(s, kind, f):
        if kind == "in":
            if first: pl.when(jnp.logical_and(s >= 0, s < ins))(f)
        else:
            pl.when(jnp.logical_and(s >= ins, s < steps))(f)
    def load(s):
        def go_in():
            grads(s, "in", "start")
            for c in moves(s, "in", 0): c.start()
        def go():
            grads(s, "layer", "start")
            for c in moves(s, "up", 0) + moves(s, "down", 0): c.start()
        on(s, "in", go_in); on(s, "layer", go)
    def stored(s):
        def go_in():
            for c in moves(s, "in", 1): c.wait()
        def go():
            for c in moves(s, "up", 1) + moves(s, "down", 1): c.wait()
        on(s, "in", go_in); on(s, "layer", go)
    for s in range(SLOTS - 1): load(jnp.int32(s))
    h[...] = jnp.zeros_like(h) if first else h_in[...]
    def step(s, _):
        sl = lax.rem(s, SLOTS)
        def upd(w, m, u, t, ix):
            nm = mu * m[(sl, *ix)] + g[sl, u, t].astype(f32)
            m[(sl, *ix)] = nm
            nw = w[(sl, *ix)] - eta * nm
            w[(sl, *ix)] = nw
            return nw.astype(bf)
        def down(lhs, u0):
            for j in range(2):
                cols = slice(j * d2, (j + 1) * d2)
                tot = h[:, cols]
                for t in range(2):
                    r = slice(t * hf // 2, (t + 1) * hf // 2)
                    tot = tot + dot(lhs(r), upd(wd, md, u0 + j, t, (r, cols)))
                h[:, cols] = tot
        def do_in():
            grads(s, "in", "wait")
            for c in moves(s, "in", 0): c.wait()
            xs = x[:, pl.ds(pl.multiple_of(s * hf, hf), hf)]
            down(lambda r: xs[:, r], 0)
            for c in moves(s, "in", 1): c.start()
        def do_layer():
            grads(s, "layer", "wait")
            for c in moves(s, "up", 0): c.wait()
            @pl.when(where(s)[1] == 0)
            def _(): p[...] = h[...].astype(bf)
            for j in range(2):
                for t in range(2):
                    cols = slice(hf // 2 * j + d2 * t, hf // 2 * j + d2 * (t + 1))
                    a[:, cols] = gelu_tanh(dot(p[...], upd(wu, mu_, j, t, (slice(None), cols)))).astype(bf)
            for c in moves(s, "up", 1): c.start()
            for c in moves(s, "down", 0): c.wait()
            down(lambda r: a[:, r], 2)
            for c in moves(s, "down", 1): c.start()
        on(s, "in", do_in); on(s, "layer", do_layer)
        stored(s - 1)
        load(s + SLOTS - 1)
        return 0
    lax.fori_loop(0, steps, step, 0)
    h_out[...] = h[...]
    if last:
        e = h[...] - y[...].astype(f32)
        loss[...] = jnp.sum(e * e, axis=1) / (2 * d)
    stored(jnp.int32(steps - 1))

def flip(v, mask, n):
    return lax.ppermute(v, "data", [(i, i ^ mask) for i in range(n)])

def update(eta, mu, x, y, g, halves, w_in, w_up, w_down, m_in, m_up, m_down, n):
    rows = x.shape[0]
    layers, d, ff = w_up.shape
    own_a, own_b, oth_a, oth_b = halves
    mid = layers - own_a.shape[0] // 8
    vm = pl.BlockSpec(memory_space=pltpu.VMEM)
    hb = pl.BlockSpec(memory_space=pl.ANY)
    sem = pltpu.SemaphoreType.DMA
    scratch = [pltpu.VMEM((SLOTS, d, ff // 2), f32)] * 2 + [pltpu.VMEM((SLOTS, ff // 2, d), f32)] * 2
    scratch += [pltpu.VMEM((SLOTS, 4, 2, 512, d // 2), bf), pltpu.VMEM((rows, d), f32), pltpu.VMEM((rows, d), bf),
                pltpu.VMEM((rows, ff // 2), bf), sem((SLOTS, 4)), sem((SLOTS, 4)), sem((SLOTS, 8))]
    params = pltpu.CompilerParams(vmem_limit_bytes=60 * 2**20)
    h_type = jax.ShapeDtypeStruct((rows, d), f32)
    def call(lo, hi, outs, ins, specs, aliases):
        c = (8 * (hi - lo) + 8 * (lo == 0)) * 512 * d
        return pl.pallas_call(
            functools.partial(upd_kernel, layers, lo, hi, eta, mu), out_shape=outs, in_specs=specs,
            out_specs=[hb if len(t.shape) > 2 or t.shape[0] > rows else vm for t in outs], scratch_shapes=scratch, compiler_params=params,
            input_output_aliases=aliases, cost_estimate=pl.CostEstimate(flops=4 * rows * c, bytes_accessed=18 * c, transcendentals=0),
            name="update_" + str(lo),
        )(*ins)
    o = [jax.ShapeDtypeStruct(t.shape, f32) for t in (w_in, w_up, w_down, m_in, m_up, m_down)]
    cut = mid - 1
    ax, bx = flip(own_a, 2, n), flip(own_b, 4, n)
    nw_in, nw_up, nw_dn, nm_in, nm_up, nm_dn, h = call(
        0, cut, o + [h_type], (x, g, w_in, w_up, w_down, m_in, m_up, m_down), [vm] + [hb] * 7, {})
    h, ax, bx = lax.optimization_barrier((h, ax, bx))
    ac, bc = flip(ax, 1, n), flip(bx, 1, n)
    mats = [o[1], o[2], o[4], o[5]]
    nw_up, nw_dn, nm_up, nm_dn, h = call(
        cut, mid, mats + [h_type], (h, g, w_up, w_down, m_up, m_down, nw_up, nw_dn, nm_up, nm_dn), [vm] + [hb] * 9,
        {6: 0, 7: 1, 8: 2, 9: 3})
    nw_up, nw_dn, nm_up, nm_dn, loss, h = call(
        mid, layers, mats + [jax.ShapeDtypeStruct((rows,), f32), h_type],
        (y, h, own_a, oth_a, ax, ac, own_b, oth_b, bx, bc, w_up, w_down, m_up, m_down, nw_up, nw_dn, nm_up, nm_dn), [vm, vm] + [hb] * 16,
        {14: 0, 15: 1, 16: 2, 17: 3})
    return nw_in, nw_up, nw_dn, nm_in, nm_up, nm_dn, loss, h

PERMUTED_LAYERS = 6

def solution(mesh):
    group_size = mesh.shape["data"]

    def device_steps(w_in, w_up, w_down, mom_in, mom_up, mom_down, x_now, y_now, x_next, y_next):
        local_rows, model_width = y_now.shape
        step_size = 4.0 * model_width / (w_up.shape[2] * (w_up.shape[0] + 1))
        part = 8 * PERMUTED_LAYERS
        def kinds(u, ty):
            odd = lax.rem(u, 2) == 1
            if ty == "late":
                return jnp.logical_and(u < part, odd)
            return jnp.logical_or(u >= part, jnp.logical_not(odd))
        total, own_a, own_b, oth_a, oth_b = gradient_sum(
            float(local_rows * group_size * model_width), x_now, y_now, w_in, w_up, w_down, part, kinds, ("late", "mid"))
        return update(step_size, MOMENTUM, x_next, y_next, total, (own_a, own_b, oth_a, oth_b), w_in, w_up, w_down, mom_in, mom_up, mom_down, group_size)

    row_spec = P("data", None)
    return jax.shard_map(
        device_steps,
        mesh=mesh,
        in_specs=(P(),) * 6 + (row_spec,) * 4,
        out_specs=(P(),) * 6 + (P("data"), row_spec),
        check_vma=False,
    )
```

time: 556 us -> 531 us (0.955)
  Pallas kernels: 555 us -> 527 us
    pallas_call x2 -> x4, Pallas kernels: 555 us -> 527 us  [the longest x1 363 us: gradient_sum(): pl.pallas_call(functools.partial(grad_sum_kernel, layers, scale, nu, part...]
  transfers between devices with their start and end apart: 0 -> 4, of which waited for: 0 -> 0; matrix products, arithmetic and copies ran while one was open for 0% -> 0% of each run, Pallas kernels for 0% -> 17%
where the time goes in v5:
time: 531 us; the launch traced here: 530 us
  Pallas kernels  527 us (99%)
    pallas_call x1, Pallas kernels, gradient_sum(): pl.pallas_call(functools.partial(grad_sum_kernel, layers, scale, nu, part...  363 us
    pallas_call x3, Pallas kernels, call(): pl.pallas_call(functools.partial(upd_kernel, layers, lo, hi, eta, mu), ou...  164 us
  transfers between devices with their start and end apart: 4, of which 0 were waited for; matrix products, arithmetic and copies ran while one was open for 0% of the time, Pallas kernels for 17%

profile of v5, /device:TPU:0, one launch (start us, length us, event | category | flops | bytes accessed | tf_op | source)
XLA Modules:
  0.0 530.5 jit_solution(7494843109706241907)
XLA Ops:
  0.6 363.2 %gradient_sum.1 = (bf16[56,2,512,256]{3,2,1,0:T(8,128)(2,1)}, bf16[48,128,256]{2,1,0:T(8,128)(2,1)}, bf16[48,128,256]{2,1,0:T(8,128)(2,1)}, bf16[48,128,256]{2,1,0:T(8,128)(2,1)}, bf16[48,128,256]{2,1,0:T(8,128)(2,1)}) custom-call(bf16[256,4096]{1,0:T(8,128)(2,1)} %refs_0_.3, bf16[256,512]{1,0:T(8,128)(2,1)} %refs_1_.1, f32[4096,512]{1,0:T(8,128)} %refs_2_.4, ...), custom_call_target="tpu_custom_call" | custom-call | tf_op jit(solution)/shard_map/gradient_sum/pallas_call | solution.py:317
  363.8 0.9 collective-permute-start
  364.8 1.2 collective-permute-start.1
  365.9 74.7 %update_0.1 = (f32[4096,512]{1,0:T(8,128)}, f32[12,512,2048]{2,1,0:T(8,128)}, f32[12,2048,512]{2,1,0:T(8,128)}, f32[4096,512]{1,0:T(8,128)}, f32[12,512,2048]{2,...) custom-call(bf16[256,4096]{1,0:T(8,128)(2,1)} %refs_0_.4, ...), custom_call_target="tpu_custom_call" | custom-call | flops 12884901888 | bytes 226492416 | tf_op jit(solution)/shard_map/update_0/pallas_call | solution.py:469
  440.6 0.0 collective-permute-done.refs_4_
  440.6 0.0 copy-start
  440.6 0.0 collective-permute-done.1.refs_8_
  440.6 0.1 collective-permute-start.2
  440.7 0.5 collective-permute-start.3
  441.2 14.5 %update_5.1 = (f32[12,512,2048]{2,1,0:T(8,128)}, f32[12,2048,512]{2,1,0:T(8,128)}, f32[12,512,2048]{2,1,0:T(8,128)}, f32[12,2048,512]{2,1,0:T(8,128)}, f32[256,512]{1,0:T(8,128)}) custom-call(f32[256,512]{1,0:T(8,128)} %get-tuple-element.39.refs_0_, ...), custom_call_target="tpu_custom_call", output_to_operand_aliasing={{0}: (6, {}), {1}: (7, {}), {2}: (8, {}), {3}: (9, {})} | custom-call | flops 2147483648 | bytes 37748736 | tf_op jit(solution)/shard_map/update_5/pallas_call | solution.py:469
  455.7 0.0 copy-done
  455.7 0.0 collective-permute-done.2.refs_5_
  455.7 0.0 collective-permute-done.3.refs_9_
  455.7 74.7 %update_6.1 = (f32[12,512,2048]{2,1,0:T(8,128)}, f32[12,2048,512]{2,1,0:T(8,128)}, f32[12,512,2048]{2,1,0:T(8,128)}, f32[12,2048,512]{2,1,0:T(8,128)}, f32[256]{0:T(256)}, /*index=5*/f32[256,512]{1,0:T(8,128)}) custom-call(bf16[256,512]{1,0:T(8,128)(2,1)} %refs_0_.5, ...), custom_call_target="tpu_custom_call", output_to_operand_aliasing={{0}: (14, {}), {1}: (15, {}), {2}: (16, {}), {3}: (17, {})} | custom-call | flops 12884901888 | bytes 226492416 | tf_op jit(solution)/shard_map/update_6/pallas_call | solution.py:469
Async XLA Ops:
  363.8 76.8 %collective-permute-start = (bf16[48,128,256]{2,1,0:T(8,128)(2,1)}, bf16[48,128,256]{2,1,0:T(8,128)(2,1)S(1)}, u32[]{:S(2)}, u32[]{:S(2)}) collective-permute-start(bf16[48,128,256]{2,1,0:T(8,128)(2,1)} %get-tuple-element.37.refs_2_), channel_id=1, source_target_pairs={{0,2},{1,3},{2,0},{3,1},{4,6},{5,7},{6,4},{7,5},{8,10},{9,11},{10,... | collective-permute-start | bytes 9437192 | tf_op jit(solution)/shard_map/ppermute | solution.py:452
  364.8 75.9 %collective-permute-start.1 = (bf16[48,128,256]{2,1,0:T(8,128)(2,1)}, bf16[48,128,256]{2,1,0:T(8,128)(2,1)}, u32[]{:S(2)}, u32[]{:S(2)}) collective-permute-start(bf16[48,128,256]{2,1,0:T(8,128)(2,1)} %get-tuple-element.38.refs_6_), channel_id=1, source_target_pairs={{0,4},{1,5},{2,6},{3,7},{4,0},{5,1},{6,2},{7,3},{8,12},{9,13},{10,... | collective-permute-start | bytes 9437192 | tf_op jit(solution)/shard_map/ppermute | solution.py:452
  440.6 15.1 %copy-start = (bf16[48,128,256]{2,1,0:T(8,128)(2,1)}, bf16[48,128,256]{2,1,0:T(8,128)(2,1)S(1)}, u32[]{:S(2)}) copy-start(bf16[48,128,256]{2,1,0:T(8,128)(2,1)S(1)} %collective-permute-done.refs_4_) | copy-start | bytes 9437188
  440.6 15.1 %collective-permute-start.2 = (bf16[48,128,256]{2,1,0:T(8,128)(2,1)S(1)}, bf16[48,128,256]{2,1,0:T(8,128)(2,1)}, u32[]{:S(2)}, u32[]{:S(2)}) collective-permute-start(bf16[48,128,256]{2,1,0:T(8,128)(2,1)S(1)} %collective-permute-done.refs_4_), channel_id=1, source_target_pairs={{0,1},{1,0},{2,3},{3,2},{4,5},{5,4},{6,7},{7,6},{8,9},{9,8},{10,11... | collective-permute-start | bytes 9437192 | tf_op jit(solution)/shard_map/ppermute | solution.py:452
  440.7 15.0 %collective-permute-start.3 = (bf16[48,128,256]{2,1,0:T(8,128)(2,1)}, bf16[48,128,256]{2,1,0:T(8,128)(2,1)}, u32[]{:S(2)}, u32[]{:S(2)}) collective-permute-start(bf16[48,128,256]{2,1,0:T(8,128)(2,1)} %collective-permute-done.1.refs_8_), channel_id=1, source_target_pairs={{0,1},{1,0},{2,3},{3,2},{4,5},{5,4},{6,7},{7,6},{8,9},{9,8},{10,11... | collective-permute-start | bytes 9437192 | tf_op jit(solution)/shard_map/ppermute | solution.py:452

commit v6 on v5

--- a/solution.py
+++ b/solution.py
@@ -328,13 +328,14 @@
     )(x, y, w_in, w_up, w_down)
 
 
-SLOTS = 4
+SLOTS, GRANTS = (4, 3, 3), (56, 44, 43)
 def upd_kernel(layers, lo, hi, eta, mu, *refs):
     scratch = refs[-11:]
     wu, mu_, wd, md, g, h, p, a, ld_s, st_s, g_s = scratch
     first, last = lo == 0, hi == layers
+    slots = wu.shape[0]
     if first:
-        x, gs, w_in, w_up, w_dn, m_in, m_up, m_dn, nw_in, nw_up, nw_dn, nm_in, nm_up, nm_dn, h_out = refs[:-11]
+        x_hbm, gs, w_in, w_up, w_dn, m_in, m_up, m_dn, nw_in, nw_up, nw_dn, nm_in, nm_up, nm_dn, h_out, x, x_s = refs[:-11]
     elif last:
         y, h_in, *pieces = refs[:10]
         w_up, w_dn, m_up, m_dn, _, _, _, _, nw_up, nw_dn, nm_up, nm_dn, loss, h_out = refs[10:-11]
@@ -348,7 +349,7 @@
         v = jnp.maximum(s - ins, 0)
         return lo + v // 2, lax.rem(v, 2)
     def moves(s, group, put):
-        sl = lax.rem(s, SLOTS)
+        sl = lax.rem(s, slots)
         if group == "in":
             at = pl.ds(pl.multiple_of(s * hf, hf), hf)
             arr = [((w_in, nw_in)[put].at[at], wd.at[sl]), ((m_in, nm_in)[put].at[at], md.at[sl])]
@@ -363,7 +364,7 @@
         sems = (ld_s, st_s)[put]
         return [pltpu.make_async_copy(*((v, hb) if put else (hb, v)), sems.at[sl, o + i]) for i, (hb, v) in enumerate(arr)]
     def grads(s, kind, what):
-        sl = lax.rem(s, SLOTS)
+        sl = lax.rem(s, slots)
         if kind == "in":
             c = pltpu.make_async_copy(gs.at[pl.ds(2 * s, 2)], g.at[sl, pl.ds(0, 2)], g_s.at[sl, 0])
             return getattr(c, what)()
@@ -379,8 +380,12 @@
             for i in range(4):
                 row = pl.multiple_of(256 * k + q * (b if i < 2 else 1 - b), q)
                 half = c if i % 2 == 0 else 1 - c
-                cp = pltpu.make_async_copy(pieces[4 * k + i].at[pl.ds(at, 4)], g.at[sl, :, half, pl.ds(row, q)], g_s.at[sl, 4 * k + i])
-                getattr(cp, what)()
+                if i < 2:
+                    cp = pltpu.make_async_copy(pieces[4 * k + i].at[pl.ds(at, 4)], g.at[sl, :, half, pl.ds(row, q)], g_s.at[sl, 4 * k + i])
+                    getattr(cp, what)()
+                elif what == "wait":
+                    for u in range(4):
+                        g[sl, u, half, pl.ds(row, q)] = pieces[4 * k + i][at + u]
     def on(s, kind, f):
         if kind == "in":
             if first: pl.when(jnp.logical_and(s >= 0, s < ins))(f)
@@ -400,10 +405,14 @@
         def go():
             for c in moves(s, "up", 1) + moves(s, "down", 1): c.wait()
         on(s, "in", go_in); on(s, "layer", go)
-    for s in range(SLOTS - 1): load(jnp.int32(s))
+    if first:
+        cp_x = pltpu.make_async_copy(x_hbm, x, x_s.at[0])
+        cp_x.start()
+    for s in range(slots - 1): load(jnp.int32(s))
+    if first: cp_x.wait()
     h[...] = jnp.zeros_like(h) if first else h_in[...]
     def step(s, _):
-        sl = lax.rem(s, SLOTS)
+        sl = lax.rem(s, slots)
         def upd(w, m, u, t, ix):
             nm = mu * m[(sl, *ix)] + g[sl, u, t].astype(f32)
             m[(sl, *ix)] = nm
@@ -439,7 +448,7 @@
             for c in moves(s, "down", 1): c.start()
         on(s, "in", do_in); on(s, "layer", do_layer)
         stored(s - 1)
-        load(s + SLOTS - 1)
+        load(s + slots - 1)
         return 0
     lax.fori_loop(0, steps, step, 0)
     h_out[...] = h[...]
@@ -459,16 +468,19 @@
     vm = pl.BlockSpec(memory_space=pltpu.VMEM)
     hb = pl.BlockSpec(memory_space=pl.ANY)
     sem = pltpu.SemaphoreType.DMA
-    scratch = [pltpu.VMEM((SLOTS, d, ff // 2), f32)] * 2 + [pltpu.VMEM((SLOTS, ff // 2, d), f32)] * 2
-    scratch += [pltpu.VMEM((SLOTS, 4, 2, 512, d // 2), bf), pltpu.VMEM((rows, d), f32), pltpu.VMEM((rows, d), bf),
-                pltpu.VMEM((rows, ff // 2), bf), sem((SLOTS, 4)), sem((SLOTS, 4)), sem((SLOTS, 8))]
-    params = pltpu.CompilerParams(vmem_limit_bytes=60 * 2**20)
+    def scratch(slots, first):
+        own_x = [pltpu.VMEM(x.shape, bf), sem((1,))] if first else []
+        return own_x + [pltpu.VMEM((slots, d, ff // 2), f32)] * 2 + [pltpu.VMEM((slots, ff // 2, d), f32)] * 2 + [
+            pltpu.VMEM((slots, 4, 2, 512, d // 2), bf), pltpu.VMEM((rows, d), f32), pltpu.VMEM((rows, d), bf),
+            pltpu.VMEM((rows, ff // 2), bf), sem((slots, 4)), sem((slots, 4)), sem((slots, 8))]
     h_type = jax.ShapeDtypeStruct((rows, d), f32)
     def call(lo, hi, outs, ins, specs, aliases):
+        which = 0 if lo == 0 else 2 if hi == layers else 1
         c = (8 * (hi - lo) + 8 * (lo == 0)) * 512 * d
         return pl.pallas_call(
             functools.partial(upd_kernel, layers, lo, hi, eta, mu), out_shape=outs, in_specs=specs,
-            out_specs=[hb if len(t.shape) > 2 or t.shape[0] > rows else vm for t in outs], scratch_shapes=scratch, compiler_params=params,
+            out_specs=[hb if len(t.shape) > 2 or t.shape[0] > rows else vm for t in outs], scratch_shapes=scratch(SLOTS[which], lo == 0),
+            compiler_params=pltpu.CompilerParams(vmem_limit_bytes=GRANTS[which] * 2**20),
             input_output_aliases=aliases, cost_estimate=pl.CostEstimate(flops=4 * rows * c, bytes_accessed=18 * c, transcendentals=0),
             name="update_" + str(lo),
         )(*ins)
@@ -476,7 +488,7 @@
     cut = mid - 1
     ax, bx = flip(own_a, 2, n), flip(own_b, 4, n)
     nw_in, nw_up, nw_dn, nm_in, nm_up, nm_dn, h = call(
-        0, cut, o + [h_type], (x, g, w_in, w_up, w_down, m_in, m_up, m_down), [vm] + [hb] * 7, {})
+        0, cut, o + [h_type], (x, g, w_in, w_up, w_down, m_in, m_up, m_down), [hb] * 8, {})
     h, ax, bx = lax.optimization_barrier((h, ax, bx))
     ac, bc = flip(ax, 1, n), flip(bx, 1, n)
     mats = [o[1], o[2], o[4], o[5]]
@@ -485,7 +497,7 @@
         {6: 0, 7: 1, 8: 2, 9: 3})
     nw_up, nw_dn, nm_up, nm_dn, loss, h = call(
         mid, layers, mats + [jax.ShapeDtypeStruct((rows,), f32), h_type],
-        (y, h, own_a, oth_a, ax, ac, own_b, oth_b, bx, bc, w_up, w_down, m_up, m_down, nw_up, nw_dn, nm_up, nm_dn), [vm, vm] + [hb] * 16,
+        (y, h, own_a, oth_a, ax, ac, own_b, oth_b, bx, bc, w_up, w_down, m_up, m_down, nw_up, nw_dn, nm_up, nm_dn), [vm] * 2 + [hb, hb, vm, vm] * 2 + [hb] * 8,
         {14: 0, 15: 1, 16: 2, 17: 3})
     return nw_in, nw_up, nw_dn, nm_in, nm_up, nm_dn, loss, h
 

time: 531 us -> 530 us (level)
  no operation moved by 1% of the time
where the time goes in v6:
time: 530 us
  Pallas kernels  523 us (99%)
    pallas_call x1, Pallas kernels, gradient_sum(): pl.pallas_call(functools.partial(grad_sum_kernel, layers, scale, nu, part...  363 us
    pallas_call x3, Pallas kernels, call(): pl.pallas_call(functools.partial(upd_kernel, layers, lo, hi, eta, mu), ou...  160 us
  transfers between devices with their start and end apart: 4, of which 0 were waited for; matrix products, arithmetic and copies ran while one was open for 0% of the time, Pallas kernels for 17%

profile of v6, /device:TPU:0, one launch (start us, length us, event | category | flops | bytes accessed | tf_op | source)
XLA Modules:
  0.0 529.6 jit_solution(16912018442403280063)
XLA Ops:
  0.6 363.2 %gradient_sum.1 = (bf16[56,2,512,256]{3,2,1,0:T(8,128)(2,1)}, bf16[48,128,256]{2,1,0:T(8,128)(2,1)}, bf16[48,128,256]{2,1,0:T(8,128)(2,1)}, bf16[48,128,256]{2,1,0:T(8,128)(2,1)}, bf16[48,128,256]{2,1,0:T(8,128)(2,1)}) custom-call(bf16[256,4096]{1,0:T(8,128)(2,1)} %refs_0_.3, bf16[256,512]{1,0:T(8,128)(2,1)} %refs_1_.1, f32[4096,512]{1,0:T(8,128)} %refs_2_.4, ...), custom_call_target="tpu_custom_call" | custom-call | tf_op jit(solution)/shard_map/gradient_sum/pallas_call | solution.py:317
  363.9 0.9 collective-permute-start
  364.8 1.2 collective-permute-start.1
  366.0 74.1 %update_0.1 = (f32[4096,512]{1,0:T(8,128)}, f32[12,512,2048]{2,1,0:T(8,128)}, f32[12,2048,512]{2,1,0:T(8,128)}, f32[4096,512]{1,0:T(8,128)}, f32[12,512,2048]{2,...) custom-call(bf16[256,4096]{1,0:T(8,128)(2,1)} %refs_0_.4, ...), custom_call_target="tpu_custom_call" | custom-call | flops 12884901888 | bytes 226492416 | tf_op jit(solution)/shard_map/update_0/pallas_call | solution.py:480
  440.1 0.0 collective-permute-done.refs_4_
  440.1 0.0 collective-permute-done.1.refs_8_
  440.1 0.0 copy-start.4
  440.1 0.1 collective-permute-start.2
  440.2 0.5 collective-permute-start.3
  440.7 0.0 copy-start.2
  440.7 1.4 copy-done.2
  442.1 0.0 copy-start
  442.1 0.0 copy-start.1
  442.1 0.0 copy-start.3
  442.1 14.0 %update_5.1 = (f32[12,512,2048]{2,1,0:T(8,128)}, f32[12,2048,512]{2,1,0:T(8,128)}, f32[12,512,2048]{2,1,0:T(8,128)}, f32[12,2048,512]{2,1,0:T(8,128)}, f32[256,512]{1,0:T(8,128)S(1)}) custom-call(f32[256,512]{1,0:T(8,128)S(1)} %copy-done.2, ...), custom_call_target="tpu_custom_call", output_to_operand_aliasing={{0}: (6, {}), {1}: (7, {}), {2}: (8, {}), {3}: (9, {})} | custom-call | flops 2147483648 | bytes 37748736 | tf_op jit(solution)/shard_map/update_5/pallas_call | solution.py:480
  456.1 0.0 copy-done.4
  456.2 0.0 collective-permute-done.2.refs_5_
  456.2 0.0 copy-start.5
  456.2 0.0 collective-permute-done.3.refs_9_
  456.2 1.6 copy-done.5
  457.8 0.0 copy-done
  457.8 0.0 copy-done.1
  457.8 0.0 copy-done.3
  457.8 71.8 %update_6.1 = (f32[12,512,2048]{2,1,0:T(8,128)}, f32[12,2048,512]{2,1,0:T(8,128)}, f32[12,512,2048]{2,1,0:T(8,128)}, f32[12,2048,512]{2,1,0:T(8,128)}, f32[256]{0:T(256)}, /*index=5*/f32[256,512]{1,0:T(8,128)}) custom-call(bf16[256,512]{1,0:T(8,128)(2,1)S(1)} %copy-done.3, ...), custom_call_target="tpu_custom_call", output_to_operand_aliasing={{0}: (14, {}), {1}: (15, {}), {2}: (16, {}), {3}: (17, {})} | custom-call | flops 12884901888 | bytes 226492416 | tf_op jit(solution)/shard_map/update_6/pallas_call | solution.py:480
Async XLA Ops:
  363.9 76.2 %collective-permute-start = (bf16[48,128,256]{2,1,0:T(8,128)(2,1)}, bf16[48,128,256]{2,1,0:T(8,128)(2,1)S(1)}, u32[]{:S(2)}, u32[]{:S(2)}) collective-permute-start(bf16[48,128,256]{2,1,0:T(8,128)(2,1)} %get-tuple-element.37.refs_2_), channel_id=1, source_target_pairs={{0,2},{1,3},{2,0},{3,1},{4,6},{5,7},{6,4},{7,5},{8,10},{9,11},{10,... | collective-permute-start | bytes 9437192 | tf_op jit(solution)/shard_map/ppermute | solution.py:461
  364.8 75.3 %collective-permute-start.1 = (bf16[48,128,256]{2,1,0:T(8,128)(2,1)}, bf16[48,128,256]{2,1,0:T(8,128)(2,1)S(1)}, u32[]{:S(2)}, u32[]{:S(2)}) collective-permute-start(bf16[48,128,256]{2,1,0:T(8,128)(2,1)} %get-tuple-element.38.refs_6_), channel_id=1, source_target_pairs={{0,4},{1,5},{2,6},{3,7},{4,0},{5,1},{6,2},{7,3},{8,12},{9,13},{10,... | collective-permute-start | bytes 9437192 | tf_op jit(solution)/shard_map/ppermute | solution.py:461
  440.1 16.0 %copy-start.4 = (bf16[48,128,256]{2,1,0:T(8,128)(2,1)}, bf16[48,128,256]{2,1,0:T(8,128)(2,1)S(1)}, u32[]{:S(2)}) copy-start(bf16[48,128,256]{2,1,0:T(8,128)(2,1)S(1)} %collective-permute-done.1.refs_8_) | copy-start | bytes 9437188
  440.1 16.0 %collective-permute-start.2 = (bf16[48,128,256]{2,1,0:T(8,128)(2,1)S(1)}, bf16[48,128,256]{2,1,0:T(8,128)(2,1)S(1)}, u32[]{:S(2)}, u32[]{:S(2)}) collective-permute-start(bf16[48,128,256]{2,1,0:T(8,128)(2,1)S(1)} %collective-permute-done.refs_4_), channel_id=1, source_target_pairs={{0,1},{1,0},{2,3},{3,2},{4,5},{5,4},{6,7},{7,6},{8,9},{9,8},{10,11... | collective-permute-start | bytes 9437192 | tf_op jit(solution)/shard_map/ppermute | solution.py:461
  440.2 16.0 %collective-permute-start.3 = (bf16[48,128,256]{2,1,0:T(8,128)(2,1)S(1)}, bf16[48,128,256]{2,1,0:T(8,128)(2,1)}, u32[]{:S(2)}, u32[]{:S(2)}) collective-permute-start(bf16[48,128,256]{2,1,0:T(8,128)(2,1)S(1)} %collective-permute-done.1.refs_8_), channel_id=1, source_target_pairs={{0,1},{1,0},{2,3},{3,2},{4,5},{5,4},{6,7},{7,6},{8,9},{9,8},{10,11... | collective-permute-start | bytes 9437192 | tf_op jit(solution)/shard_map/ppermute | solution.py:461
  440.7 1.4 copy-start.2
  442.1 15.7 %copy-start = (bf16[48,128,256]{2,1,0:T(8,128)(2,1)S(1)}, bf16[48,128,256]{2,1,0:T(8,128)(2,1)}, u32[]{:S(2)}) copy-start(bf16[48,128,256]{2,1,0:T(8,128)(2,1)} %get-tuple-element.37.refs_2_) | copy-start | bytes 9437188
  442.1 15.7 %copy-start.1 = (bf16[48,128,256]{2,1,0:T(8,128)(2,1)S(1)}, bf16[48,128,256]{2,1,0:T(8,128)(2,1)}, u32[]{:S(2)}) copy-start(bf16[48,128,256]{2,1,0:T(8,128)(2,1)} %get-tuple-element.45.refs_3_) | copy-start | bytes 9437188
  442.1 15.7 %copy-start.3 = (bf16[256,512]{1,0:T(8,128)(2,1)S(1)}, bf16[256,512]{1,0:T(8,128)(2,1)}, u32[]{:S(2)}) copy-start(bf16[256,512]{1,0:T(8,128)(2,1)} %refs_0_.5) | copy-start | bytes 786436
  456.2 1.6 copy-start.5

commit v7 on v6

--- a/solution.py
+++ b/solution.py
@@ -328,7 +328,7 @@
     )(x, y, w_in, w_up, w_down)
 
 
-SLOTS, GRANTS = (4, 3, 3), (56, 44, 43)
+SLOTS, GRANTS = (4, 3, 3), (52, 44, 43)
 def upd_kernel(layers, lo, hi, eta, mu, *refs):
     scratch = refs[-11:]
     wu, mu_, wd, md, g, h, p, a, ld_s, st_s, g_s = scratch

time: 530 us -> 528 us (level)
  no operation moved by 1% of the time
where the time goes in v7:
time: 528 us
  Pallas kernels  523 us (99%)
    pallas_call x1, Pallas kernels, gradient_sum(): pl.pallas_call(functools.partial(grad_sum_kernel, layers, scale, nu, part...  363 us
    pallas_call x3, Pallas kernels, call(): pl.pallas_call(functools.partial(upd_kernel, layers, lo, hi, eta, mu), ou...  160 us
  transfers between devices with their start and end apart: 4, of which 0 were waited for; matrix products, arithmetic and copies ran while one was open for 0% of the time, Pallas kernels for 17%

profile of v7, /device:TPU:0, one launch (start us, length us, event | category | flops | bytes accessed | tf_op | source)
XLA Modules:
  0.0 527.9 jit_solution(16321298508004343616)
XLA Ops:
  0.6 363.2 %gradient_sum.1 = (bf16[56,2,512,256]{3,2,1,0:T(8,128)(2,1)}, bf16[48,128,256]{2,1,0:T(8,128)(2,1)}, bf16[48,128,256]{2,1,0:T(8,128)(2,1)}, bf16[48,128,256]{2,1,0:T(8,128)(2,1)}, bf16[48,128,256]{2,1,0:T(8,128)(2,1)}) custom-call(bf16[256,4096]{1,0:T(8,128)(2,1)} %refs_0_.3, bf16[256,512]{1,0:T(8,128)(2,1)} %refs_1_.1, f32[4096,512]{1,0:T(8,128)} %refs_2_.4, ...), custom_call_target="tpu_custom_call" | custom-call | tf_op jit(solution)/shard_map/gradient_sum/pallas_call | solution.py:317
  363.9 0.9 collective-permute-start
  364.8 1.2 collective-permute-start.1
  366.0 73.3 %update_0.1 = (f32[4096,512]{1,0:T(8,128)}, f32[12,512,2048]{2,1,0:T(8,128)}, f32[12,2048,512]{2,1,0:T(8,128)}, f32[4096,512]{1,0:T(8,128)}, f32[12,512,2048]{2,...) custom-call(bf16[256,4096]{1,0:T(8,128)(2,1)} %refs_0_.4, ...), custom_call_target="tpu_custom_call" | custom-call | flops 12884901888 | bytes 226492416 | tf_op jit(solution)/shard_map/update_0/pallas_call | solution.py:480
  439.3 0.0 collective-permute-done.refs_4_
  439.3 0.0 collective-permute-done.1.refs_8_
  439.3 0.0 copy-start.3
  439.3 0.1 collective-permute-start.2
  439.4 0.5 collective-permute-start.3
  439.9 0.0 copy-start
  439.9 0.0 copy-start.1
  439.9 0.0 copy-start.2
  439.9 14.5 %update_5.1 = (f32[12,512,2048]{2,1,0:T(8,128)}, f32[12,2048,512]{2,1,0:T(8,128)}, f32[12,512,2048]{2,1,0:T(8,128)}, f32[12,2048,512]{2,1,0:T(8,128)}, f32[256,512]{1,0:T(8,128)S(1)}) custom-call(f32[256,512]{1,0:T(8,128)S(1)} %get-tuple-element.39.refs_0_, ...), custom_call_target="tpu_custom_call", output_to_operand_aliasing={{0}: (6, {}), {1}: (7, {}), {2}: (8, {}), {3}: (9, {})} | custom-call | flops 2147483648 | bytes 37748736 | tf_op jit(solution)/shard_map/update_5/pallas_call | solution.py:480
  454.5 0.0 copy-done.3
  454.5 0.0 collective-permute-done.2.refs_5_
  454.5 0.0 copy-start.4
  454.5 0.0 collective-permute-done.3.refs_9_
  454.5 1.6 copy-done.4
  456.1 0.0 copy-done
  456.1 0.0 copy-done.1
  456.1 0.0 copy-done.2
  456.1 71.8 %update_6.1 = (f32[12,512,2048]{2,1,0:T(8,128)}, f32[12,2048,512]{2,1,0:T(8,128)}, f32[12,512,2048]{2,1,0:T(8,128)}, f32[12,2048,512]{2,1,0:T(8,128)}, f32[256]{0:T(256)}, /*index=5*/f32[256,512]{1,0:T(8,128)}) custom-call(bf16[256,512]{1,0:T(8,128)(2,1)S(1)} %copy-done.2, ...), custom_call_target="tpu_custom_call", output_to_operand_aliasing={{0}: (14, {}), {1}: (15, {}), {2}: (16, {}), {3}: (17, {})} | custom-call | flops 12884901888 | bytes 226492416 | tf_op jit(solution)/shard_map/update_6/pallas_call | solution.py:480
Async XLA Ops:
  363.9 75.4 %collective-permute-start = (bf16[48,128,256]{2,1,0:T(8,128)(2,1)}, bf16[48,128,256]{2,1,0:T(8,128)(2,1)S(1)}, u32[]{:S(2)}, u32[]{:S(2)}) collective-permute-start(bf16[48,128,256]{2,1,0:T(8,128)(2,1)} %get-tuple-element.37.refs_2_), channel_id=1, source_target_pairs={{0,2},{1,3},{2,0},{3,1},{4,6},{5,7},{6,4},{7,5},{8,10},{9,11},{10,... | collective-permute-start | bytes 9437192 | tf_op jit(solution)/shard_map/ppermute | solution.py:461
  364.8 74.5 %collective-permute-start.1 = (bf16[48,128,256]{2,1,0:T(8,128)(2,1)}, bf16[48,128,256]{2,1,0:T(8,128)(2,1)S(1)}, u32[]{:S(2)}, u32[]{:S(2)}) collective-permute-start(bf16[48,128,256]{2,1,0:T(8,128)(2,1)} %get-tuple-element.38.refs_6_), channel_id=1, source_target_pairs={{0,4},{1,5},{2,6},{3,7},{4,0},{5,1},{6,2},{7,3},{8,12},{9,13},{10,... | collective-permute-start | bytes 9437192 | tf_op jit(solution)/shard_map/ppermute | solution.py:461
  439.3 15.1 %copy-start.3 = (bf16[48,128,256]{2,1,0:T(8,128)(2,1)}, bf16[48,128,256]{2,1,0:T(8,128)(2,1)S(1)}, u32[]{:S(2)}) copy-start(bf16[48,128,256]{2,1,0:T(8,128)(2,1)S(1)} %collective-permute-done.1.refs_8_) | copy-start | bytes 9437188
  439.3 15.1 %collective-permute-start.2 = (bf16[48,128,256]{2,1,0:T(8,128)(2,1)S(1)}, bf16[48,128,256]{2,1,0:T(8,128)(2,1)S(1)}, u32[]{:S(2)}, u32[]{:S(2)}) collective-permute-start(bf16[48,128,256]{2,1,0:T(8,128)(2,1)S(1)} %collective-permute-done.refs_4_), channel_id=1, source_target_pairs={{0,1},{1,0},{2,3},{3,2},{4,5},{5,4},{6,7},{7,6},{8,9},{9,8},{10,11... | collective-permute-start | bytes 9437192 | tf_op jit(solution)/shard_map/ppermute | solution.py:461
  439.4 15.1 %collective-permute-start.3 = (bf16[48,128,256]{2,1,0:T(8,128)(2,1)S(1)}, bf16[48,128,256]{2,1,0:T(8,128)(2,1)}, u32[]{:S(2)}, u32[]{:S(2)}) collective-permute-start(bf16[48,128,256]{2,1,0:T(8,128)(2,1)S(1)} %collective-permute-done.1.refs_8_), channel_id=1, source_target_pairs={{0,1},{1,0},{2,3},{3,2},{4,5},{5,4},{6,7},{7,6},{8,9},{9,8},{10,11... | collective-permute-start | bytes 9437192 | tf_op jit(solution)/shard_map/ppermute | solution.py:461
  439.9 16.2 %copy-start = (bf16[48,128,256]{2,1,0:T(8,128)(2,1)S(1)}, bf16[48,128,256]{2,1,0:T(8,128)(2,1)}, u32[]{:S(2)}) copy-start(bf16[48,128,256]{2,1,0:T(8,128)(2,1)} %get-tuple-element.37.refs_2_) | copy-start | bytes 9437188
  439.9 16.2 %copy-start.1 = (bf16[48,128,256]{2,1,0:T(8,128)(2,1)S(1)}, bf16[48,128,256]{2,1,0:T(8,128)(2,1)}, u32[]{:S(2)}) copy-start(bf16[48,128,256]{2,1,0:T(8,128)(2,1)} %get-tuple-element.45.refs_3_) | copy-start | bytes 9437188
  439.9 16.2 %copy-start.2 = (bf16[256,512]{1,0:T(8,128)(2,1)S(1)}, bf16[256,512]{1,0:T(8,128)(2,1)}, u32[]{:S(2)}) copy-start(bf16[256,512]{1,0:T(8,128)(2,1)} %refs_0_.5) | copy-start | bytes 786436
  454.5 1.6 copy-start.4
